TPU v7x, 32 devices: a whole 2x2x4 slice. The times are simulated.
32 devices in a mesh: dp: 8 (over y, x, core), tensor: 4 (over z).
Axes of the slice: x: 2, y: 2, z: 4, core: 2. Of those that a mesh axis runs over, the one named last changes fastest.
Arguments:
- inputs: bfloat16 [584, 16, 1024], P('tensor', 'dp'), may hold values from -6 to 6
- valid_mask: int32 [16, 584], P('dp'), may hold values from 0 to 1, as said below
- cotangent: bfloat16 [584, 16, 1024], P('tensor', 'dp'), may hold values from -60 to 60
- ln_gain: bfloat16 [2, 1024], P(None, 'dp'), may hold values from 0.25 to 1.75
- d_bias: bfloat16 [4, 1024], P(None, 'dp'), may hold values from -3 to 3
- w_qkv: bfloat16 [1024, 3, 1024], P('dp', None, 'tensor'), may hold values from -0.1875 to 0.1875
- b_qv: bfloat16 [2, 1024], P(None, 'tensor'), may hold values from -3 to 3
- w_o: bfloat16 [1024, 1024], P('tensor', 'dp'), may hold values from -2 to 2
- w_1: bfloat16 [1024, 4096], P('dp', 'tensor'), may hold values from -0.1875 to 0.1875
- b_1: bfloat16 [4096], P('tensor'), may hold values from -3 to 3
- w_2: bfloat16 [4096, 1024], P('tensor', 'dp'), may hold values from -0.09375 to 0.09375
Outputs:
- block_output: bfloat16 [584, 16, 1024], P('tensor', 'dp')
- grad_inputs: float32 [584, 16, 1024], P('tensor', 'dp')
- grad_ln_gain: float32 [2, 1024], P(None, 'dp')
- grad_d_bias: float32 [4, 1024], P(None, 'dp')
- grad_w_qkv: float32 [1024, 3, 1024], P('dp', None, 'tensor')
- grad_b_qv: float32 [2, 1024], P(None, 'tensor')
- grad_w_o: float32 [1024, 1024], P('tensor', 'dp')
- grad_w_1: float32 [1024, 4096], P('dp', 'tensor')
- grad_b_1: float32 [4096], P('tensor')
- grad_w_2: float32 [4096, 1024], P('tensor', 'dp')
Inputs may be any that keep to these rules, and one draw needn't show every extreme that they name: `valid_mask`: each image has exactly 577 positions marked 1, the others 0.
All inputs are finite; a program needn't handle non-finite values.
Results may differ from a plain program's by a relative error of at most 0.017.
Values may be sent and summed in bfloat16 or wider, within the bound.
A program may use at most 128 MiB of HBM per device.

v0:
```python
import functools

import jax
import jax.numpy as jnp
from jax import lax
from jax.experimental import pallas as pl
from jax.experimental.pallas import tpu as pltpu
from jax.sharding import PartitionSpec as P

HD = 64


EPSILON = 1e-06
MASKED = -1e30


def layer_norm(values, gain, shift):
    average = jnp.mean(values, axis=-1, keepdims=True)
    centred = values - average
    variance = jnp.mean(centred * centred, axis=-1, keepdims=True)
    return centred * lax.rsqrt(variance + EPSILON) * gain + shift


def gelu_exact(values):
    return jax.nn.gelu(values, approximate=False)


def gather_layer(ln_gain, d_bias, w_qkv, w_o, w_1, w_2):
    return (
        lax.all_gather(ln_gain, "dp", axis=1, tiled=True),
        lax.all_gather(d_bias, "dp", axis=1, tiled=True),
        lax.all_gather(w_qkv, "dp", axis=0, tiled=True),
        lax.all_gather(w_o, "dp", axis=1, tiled=True),
        lax.all_gather(w_1, "dp", axis=0, tiled=True),
        lax.all_gather(w_2, "dp", axis=1, tiled=True),
    )


def masked_scores(queries, keys_part, valid):
    scores = jnp.einsum(
        "qhd,khd->hqk", queries, keys_part, preferred_element_type=jnp.float32
    ) * HD ** (-0.5)
    return jnp.where(valid[None, None, :] > 0, scores, MASKED)


def attend_forward(bundle):
    packed, valid = bundle
    scores = masked_scores(packed[:, 0], packed[:, 1], valid)
    highest = jnp.max(scores, axis=-1, keepdims=True)
    exponent = jnp.exp(scores - highest)
    denominator = jnp.sum(exponent, axis=-1, keepdims=True)
    attention = (exponent / denominator).astype(jnp.bfloat16)
    mixture = jnp.einsum(
        "hqk,khd->qhd", attention, packed[:, 2], preferred_element_type=jnp.float32
    )
    return (mixture.astype(jnp.bfloat16), (highest + jnp.log(denominator))[..., 0])


def attend_backward(bundle):
    packed, grad_mixture, log_total, valid = bundle
    queries = packed[:, 0]
    keys_part = packed[:, 1]
    values_part = packed[:, 2]
    scores = masked_scores(queries, keys_part, valid)
    attention = jnp.exp(scores - log_total[..., None])
    attention_low = attention.astype(jnp.bfloat16)
    grad_values = jnp.einsum(
        "hqk,qhd->khd", attention_low, grad_mixture, preferred_element_type=jnp.float32
    )
    grad_attention = jnp.einsum(
        "qhd,khd->hqk", grad_mixture, values_part, preferred_element_type=jnp.float32
    )
    inner = jnp.sum(attention * grad_attention, axis=-1, keepdims=True)
    grad_scores = (attention * (grad_attention - inner)).astype(jnp.bfloat16)
    factor = HD ** (-0.5)
    grad_queries = (
        jnp.einsum("hqk,khd->qhd", grad_scores, keys_part, preferred_element_type=jnp.float32)
        * factor
    )
    grad_keys = (
        jnp.einsum("hqk,qhd->khd", grad_scores, queries, preferred_element_type=jnp.float32)
        * factor
    )
    return jnp.stack([grad_queries, grad_keys, grad_values], axis=1)


def body(inputs, valid_mask, cotangent, ln_gain, d_bias, w_qkv, b_qv, w_o, w_1, b_1, w_2):
    local_rows, images, model_width = inputs.shape
    layer = gather_layer(ln_gain, d_bias, w_qkv, w_o, w_1, w_2)
    gains = layer[0].astype(jnp.float32)
    shifts = layer[1].astype(jnp.float32)
    wide_qkv = layer[2].reshape(model_width, -1)
    wide_out = layer[3]
    wide_up = layer[4]
    wide_down = layer[5]
    residual = inputs.astype(jnp.float32)
    normed1 = layer_norm(residual, gains[0], shifts[0]).astype(jnp.bfloat16)
    gathered1 = lax.all_gather(normed1, "tensor", axis=0, tiled=True)
    full_length = gathered1.shape[0]
    columns = b_qv.shape[1]
    heads_local = columns // HD
    projected = jnp.dot(gathered1, wide_qkv, preferred_element_type=jnp.float32).reshape(
        full_length, images, 3, columns
    )
    qkv_bias = jnp.stack([b_qv[0], jnp.zeros_like(b_qv[0]), b_qv[1]]).astype(jnp.float32)
    projected_low = (projected + qkv_bias).astype(jnp.bfloat16)
    per_image = jnp.transpose(projected_low, (1, 0, 2, 3)).reshape(
        images, full_length, 3, heads_local, HD
    )
    mixture, log_total = lax.map(attend_forward, (per_image, valid_mask))
    mixture_seq = jnp.transpose(mixture, (1, 0, 2, 3)).reshape(full_length, images, columns)
    segment = mixture_seq
    attn_sum = lax.psum_scatter(
        jnp.dot(segment, wide_out, preferred_element_type=jnp.float32),
        "tensor",
        scatter_dimension=0,
        tiled=True,
    )
    hidden1 = residual + attn_sum + shifts[2]
    normed2 = layer_norm(hidden1, gains[1], shifts[1]).astype(jnp.bfloat16)
    gathered2 = lax.all_gather(normed2, "tensor", axis=0, tiled=True)
    hidden_in = jnp.dot(gathered2, wide_up, preferred_element_type=jnp.float32) + b_1.astype(
        jnp.float32
    )
    active = gelu_exact(hidden_in).astype(jnp.bfloat16)
    segment = active
    branch_sum = lax.psum_scatter(
        jnp.dot(segment, wide_down, preferred_element_type=jnp.float32).astype(jnp.bfloat16),
        "tensor",
        scatter_dimension=0,
        tiled=True,
    ).astype(jnp.float32)
    block_output = (hidden1 + branch_sum + shifts[3]).astype(jnp.bfloat16)
    layer = gather_layer(ln_gain, d_bias, w_qkv, w_o, w_1, w_2)
    wide_qkv = layer[2].reshape(model_width, -1)
    wide_out = layer[3]
    wide_up = layer[4]
    wide_down = layer[5]
    grad_out = cotangent.astype(jnp.float32)
    grad_gathered = lax.all_gather(cotangent, "tensor", axis=0, tiled=True)
    grad_w_2 = jnp.einsum("sif,sid->fd", active, grad_gathered, preferred_element_type=jnp.float32)
    grad_active = jnp.einsum(
        "sid,fd->sif", grad_gathered, wide_down, preferred_element_type=jnp.float32
    )
    grad_hidden_in = jax.vjp(gelu_exact, hidden_in)[1](grad_active)[0]
    grad_b_1 = jnp.sum(grad_hidden_in, axis=(0, 1))
    grad_hidden_low = grad_hidden_in.astype(jnp.bfloat16)
    grad_w_1 = jnp.einsum(
        "sid,sif->df", gathered2, grad_hidden_low, preferred_element_type=jnp.float32
    )
    segment = grad_hidden_low
    grad_normed2 = lax.psum_scatter(
        jnp.einsum("sif,df->sid", segment, wide_up, preferred_element_type=jnp.float32),
        "tensor",
        scatter_dimension=0,
        tiled=True,
    )
    second_pull = jax.vjp(layer_norm, hidden1, gains[1], shifts[1])[1]
    grad_from_norm, gain2_grad, shift2_grad = second_pull(grad_normed2)
    grad_hidden1 = grad_out + grad_from_norm
    grad_attn_low = grad_hidden1.astype(jnp.bfloat16)
    grad_attn_all = lax.all_gather(grad_attn_low, "tensor", axis=0, tiled=True)
    grad_w_o = jnp.einsum(
        "sic,sid->cd", mixture_seq, grad_attn_all, preferred_element_type=jnp.float32
    )
    grad_mixture = jnp.einsum(
        "sid,cd->sic", grad_attn_all, wide_out, preferred_element_type=jnp.float32
    ).astype(jnp.bfloat16)
    grad_mixture_img = jnp.transpose(
        grad_mixture.reshape(full_length, images, heads_local, HD), (1, 0, 2, 3)
    )
    grad_packed = lax.map(attend_backward, (per_image, grad_mixture_img, log_total, valid_mask))
    grad_projected = jnp.transpose(grad_packed, (1, 0, 2, 3, 4)).reshape(
        full_length, images, 3, columns
    )
    grad_b_qv = jnp.stack(
        [
            jnp.sum(grad_projected[:, :, 0], axis=(0, 1)),
            jnp.sum(grad_projected[:, :, 2], axis=(0, 1)),
        ]
    )
    grad_projected_low = grad_projected.reshape(full_length, images, 3 * columns).astype(
        jnp.bfloat16
    )
    grad_w_qkv = jnp.einsum(
        "sid,sic->dc", gathered1, grad_projected_low, preferred_element_type=jnp.float32
    ).reshape(model_width, 3, columns)
    segment = grad_projected_low
    grad_normed1 = lax.psum_scatter(
        jnp.einsum("sic,dc->sid", segment, wide_qkv, preferred_element_type=jnp.float32).astype(
            jnp.bfloat16
        ),
        "tensor",
        scatter_dimension=0,
        tiled=True,
    ).astype(jnp.float32)
    first_pull = jax.vjp(layer_norm, residual, gains[0], shifts[0])[1]
    grad_from_front, gain1_grad, shift1_grad = first_pull(grad_normed1)
    grad_inputs = grad_hidden1 + grad_from_front
    gain_terms = jnp.stack([gain1_grad, gain2_grad])
    shift_terms = jnp.stack(
        [
            shift1_grad,
            shift2_grad,
            jnp.sum(grad_hidden1, axis=(0, 1)),
            jnp.sum(grad_out, axis=(0, 1)),
        ]
    )
    scattered = (
        lax.psum_scatter(
            gain_terms.astype(jnp.bfloat16), "dp", scatter_dimension=1, tiled=True
        ).astype(jnp.float32),
        lax.psum_scatter(
            shift_terms.astype(jnp.bfloat16), "dp", scatter_dimension=1, tiled=True
        ).astype(jnp.float32),
        lax.psum_scatter(
            grad_w_qkv.astype(jnp.bfloat16), "dp", scatter_dimension=0, tiled=True
        ).astype(jnp.float32),
        lax.psum_scatter(
            grad_w_o.astype(jnp.bfloat16), "dp", scatter_dimension=1, tiled=True
        ).astype(jnp.float32),
        lax.psum_scatter(
            grad_w_1.astype(jnp.bfloat16), "dp", scatter_dimension=0, tiled=True
        ).astype(jnp.float32),
        lax.psum_scatter(
            grad_w_2.astype(jnp.bfloat16), "dp", scatter_dimension=1, tiled=True
        ).astype(jnp.float32),
    )
    gain_sum, shift_sum = lax.psum((scattered[0], scattered[1]), "tensor")
    bias_qv_sum, bias_up_sum = lax.psum((grad_b_qv, grad_b_1), "dp")
    return (
        block_output,
        grad_inputs,
        gain_sum,
        shift_sum,
        scattered[2],
        bias_qv_sum,
        scattered[3],
        scattered[4],
        bias_up_sum,
        scattered[5],
    )


Q = 160
HALF = 2 * Q
FULL = 4 * Q
BF, F32 = jnp.bfloat16, jnp.float32
MESH = pl.DeviceIdType.MESH


def place(y, x, c, z):
    return (y * 4 + x * 2 + c, z)


def at_rows(start, size, step=8):
    return pl.ds(pl.multiple_of(start, step), size)


def mm(left, right, dims):
    return lax.dot_general(left, right, (dims, ((), ())), preferred_element_type=F32)


NN = ((1,), (0,))
NT = ((1,), (1,))
TN = ((0,), (0,))


class Links:
    def __init__(self, send_sem, recv_sem):
        self.send_sem, self.recv_sem = send_sem, recv_sem
        self.sends, self.used, self.keys, self.dropped = [], 0, {}, set()

    def base(self, key, count):
        if key not in self.keys:
            self.keys[key] = self.used
            self.used += count
        return self.keys[key]

    def copy(self, src, dst, sent, got, to):
        return pltpu.make_async_remote_copy(
            src_ref=src,
            dst_ref=dst,
            send_sem=self.send_sem.at[sent],
            recv_sem=self.recv_sem.at[got],
            device_id=to,
            device_id_type=MESH,
        )

    def drop(self, *sent):
        self.dropped = self.dropped | set(sent)

    def each(self, make, act):
        src, dst, sent, got, to, when = make()
        if when is None:
            act(self.copy(src, dst, sent, got, to))
        else:
            pl.when(when)(lambda: act(self.copy(src, dst, sent, got, to)))

    def start(self, make):
        self.sends.append(make)
        self.each(make, lambda copy: copy.start())

    def put(self, src, dst, sent, got, to, when=None):
        self.start(lambda: (src, dst, sent, got, to, when))

    def wait(self, dst, got, to):
        self.copy(dst, dst, 0, got, to).wait_recv()

    def finish(self):
        for make in self.sends:
            sent = make()[2]
            if not (isinstance(sent, int) and sent in self.dropped):
                self.each(make, lambda copy: copy.wait_send())


def where_am_i():
    d = lax.axis_index("dp")
    return d // 4, (d // 2) % 2, d % 2, lax.axis_index("tensor")


def greet(y, x, c, z):
    barrier = pltpu.get_barrier_semaphore()
    peers = [(dy, dx, dc, 0) for dy in range(2) for dx in range(2) for dc in range(2) if dy + dx + dc]
    peers += [(0, 0, dc, dz) for dc in range(2) for dz in range(1, 4)]
    for dy, dx, dc, dz in peers:
        to = place((y + dy) % 2, (x + dx) % 2, (c + dc) % 2, (z + dz) % 4)
        pl.semaphore_signal(barrier, inc=1, device_id=to, device_id_type=MESH)
    pl.semaphore_wait(barrier, len(peers))


def unit_rows(v):
    average = jnp.mean(v, axis=-1, keepdims=True)
    centred = v - average
    variance = jnp.mean(centred * centred, axis=-1, keepdims=True)
    scale = lax.rsqrt(variance + EPSILON)
    return centred * scale, scale


def gelu_both(v):
    cdf = 0.5 * (1.0 + lax.erf(v * 0.7071067811865476))
    density = 0.3989422804014327 * jnp.exp(-0.5 * v * v)
    return v * cdf, cdf + v * density


def layer_kernel(
    tok_in, cot_in, mask_in, norm_in, bias_in, qkv_in, wo_in, w1_in, w2_in,
    block_out, grad_out, sums_out, qv_out, b1_out, qkv_out, wo_out, w1_out, w2_out,
    tok, cot, mask, norm, bias, qkv, wo, up, down,
    n1, proj, lse, mix, hid, n2, act, slope,
    norm_row, qkv_row, up_row, part, got_part,
    ga, gmix, gproj, d_up, d_down, d_qkv, d_wo, r_up, r_down, z_up, z_down, f_up, f_down, o_up, o_down,
    first_qkv, first_wo, second_qkv, second_wo, z_qkv, z_wo, f_qkv, f_wo, o_qkv, o_wo,
    s_far, s_mid, s_near, g_far, g_mid, g_near, b_far, b_mid, b_near, g_n1,
    sums, sums_row, sums_got, sums_z, gb1, gbq, gbv, bias_pack, bias_got, bias_all,
    local_sem, send_sem, recv_sem,
):
    y, x, c, z = where_am_i()
    r = y * 2 + x
    links = Links(send_sem, recv_sem)
    me = place(y, x, c, z)
    to_c, to_x, to_y = place(y, x, 1 - c, z), place(y, 1 - x, c, z), place(1 - y, x, c, z)
    up_z, down_z = place(y, x, c, jnp.minimum(z + 1, 3)), place(y, x, c, jnp.maximum(z - 1, 0))
    greet(y, x, c, z)

    block_at = lambda ref, t: ref.at[at_rows(t * HALF, HALF, 64), :]
    block_rows = lambda t, start, size: at_rows(t * HALF + start, size, 32)

    def local(at, src, dst):
        return pltpu.make_async_copy(src, dst, local_sem.at[at])

    qkv_at = lambda rr, zz: qkv.at[at_rows(rr * 256, 256, 256), at_rows(zz * 384, 384, 128)]
    wo_at = lambda rr, zz: wo.at[at_rows(zz * 128, 128, 128), at_rows(rr * 256, 256, 128)]
    qkv_shard = qkv.at[at_rows(r * 256 + c * 128, 128, 128), at_rows(z * 384, 384, 128)]
    wo_shard = wo.at[at_rows(z * 128, 128, 128), at_rows(r * 256 + c * 128, 128, 128)]
    qkv_other = qkv.at[at_rows(r * 256 + (1 - c) * 128, 128, 128), at_rows(z * 384, 384, 128)]
    wo_other = wo.at[at_rows(z * 128, 128, 128), at_rows(r * 256 + (1 - c) * 128, 128, 128)]
    s_pc = links.base("pc", 2)
    links.put(qkv_in.at[:, at_rows((1 - c) * 384, 384, 128)], qkv_shard, s_pc, s_pc, to_c)
    links.put(wo_in.at[at_rows((1 - c) * 128, 128, 128), :], wo_shard, s_pc + 1, s_pc + 1, to_c)
    own_qkv = local(0, qkv_in.at[:, at_rows(c * 384, 384, 128)], qkv_shard)
    own_wo = local(1, wo_in.at[at_rows(c * 128, 128, 128), :], wo_shard)
    own_qkv.start()
    own_wo.start()

    s_norm, s_bias, s_mask = links.base("norm", 8), links.base("bias", 4), links.base("mask", 1)
    d = y * 4 + x * 2 + c
    for dd in range(1, 8):
        to = place((y + dd // 4) % 2, (x + (dd // 2) % 2) % 2, (c + dd % 2) % 2, z)
        links.put(norm_in, norm.at[d], s_norm + dd, s_norm + dd, to)
    for dz in range(1, 4):
        links.put(bias_in, bias.at[z], s_bias + dz, s_bias + dz, place(y, x, c, (z + dz) % 4))
    links.put(mask_in, mask.at[c], s_mask, s_mask, to_c)
    own_small = (local(2, norm_in, norm.at[d]), local(3, bias_in, bias.at[z]), local(4, mask_in, mask.at[c]))
    for one in own_small:
        one.start()

    def move_tokens(key, source, target_at, at):
        base = links.base(key, 4)
        target = target_at(z // 2)
        stay = c == z // 2
        rows = at_rows((z % 2) * Q, Q, 16)
        for i in range(2):
            here = jnp.logical_and(stay, z % 2 == i)
            to = place(y, x, z // 2, 2 * c + i)
            to = (jnp.where(here, place(y, x, 1 - c, z)[0], to[0]), to[1])
            links.put(source.at[i], target.at[rows], base + i, base + 2 + z % 2, to, jnp.logical_not(here))

            @pl.when(here)
            def _(i=i):
                local(at, source.at[i], target.at[rows]).start()

    def wait_tokens(key, source, target_at, at):
        base = links.base(key, 4)
        target = target_at(c)
        stay = c == z // 2
        for j in range(2):
            here = jnp.logical_and(stay, z % 2 == j)

            @pl.when(here)
            def _(j=j):
                local(at, source.at[j], target.at[pl.ds(j * Q, Q)]).wait()

            @pl.when(jnp.logical_not(here))
            def _(j=j):
                links.wait(target.at[pl.ds(j * Q, Q)], base + 2 + j, to_c)

    move_tokens("tok", tok_in, lambda cc: tok, 5)

    up_shard = lambda sx, sc: up.at[at_rows(y * 512 + sx * 256 + sc * 128, 128, 128), at_rows(z * 256, 256, 128)]
    down_shard = lambda sx, sc: down.at[at_rows(z * 256, 256, 128), at_rows(y * 512 + sx * 256 + sc * 128, 128, 128)]
    s_up, s_down = links.base("up", 4), links.base("down", 4)
    q = 2 * x + c
    for dx, dc in ((1, 0), (1, 1), (0, 1)):
        tx, tc = (x + dx) % 2, (c + dc) % 2
        to, rel = place(y, tx, tc, z), 2 * dx + dc
        links.put(w1_in.at[:, at_rows((2 * tx + tc) * 256, 256, 128)], up_shard(x, c), s_up + rel, s_up + rel, to)
        links.put(w2_in.at[at_rows((2 * tx + tc) * 256, 256, 128), :], down_shard(x, c), s_down + rel, s_down + rel, to)
    own_up = local(6, w1_in.at[:, at_rows(q * 256, 256, 128)], up_shard(x, c))
    own_down = local(7, w2_in.at[at_rows(q * 256, 256, 128), :], down_shard(x, c))
    own_up.start()
    own_down.start()

    class Line:
        def __init__(self, key, piece, arrived):
            self.piece, self.arrived = piece, arrived
            self.many = many = len(piece(0))
            self.got = [links.base((key, "got", n), 4) for n in range(many)]
            self.up = [links.base((key, "up", n), 4) for n in range(many)]
            self.down = [links.base((key, "down", n), 4) for n in range(many)]

        def push(self, way_up, far):
            def make(n):
                o, there = self.origin(way_up, far)
                ref = self.piece(o)[n]
                sent = (self.up if way_up else self.down)[n] + o
                onward = z < 3 if way_up else z > 0
                when = onward if there is None else jnp.logical_and(there, onward)
                return ref, ref, sent, self.got[n] + o, up_z if way_up else down_z, when

            for n in range(self.many):
                links.start(functools.partial(make, n))

        def origin(self, way_up, far):
            if far == 0:
                return z, None
            o = z - far if way_up else z + far
            return jnp.clip(o, 0, 3), (o >= 0 if way_up else o < 4)

        def begin(self):
            self.push(True, 0)
            self.push(False, 0)
            self.arrived(functools.partial(self.origin, True, 0))

        def step(self, far):
            for way_up in (True, False):
                o, there = self.origin(way_up, far)

                @pl.when(there)
                def _():
                    for n, ref in enumerate(self.piece(o)):
                        links.wait(ref, self.got[n] + o, up_z)

                self.push(way_up, far)
                self.arrived(functools.partial(self.origin, way_up, far))

    s_first = [links.base(("first", n), 4) for n in range(2)]
    s_own = [links.base(("own", n), 4) for n in range(2)]
    s_fwd = [links.base(("fwd", n), 4) for n in range(2)]

    def neighbours(o):
        odd = o % 2
        even = 1 - odd
        y1, x1 = y + odd * (1 - 2 * y), x + even * (1 - 2 * x)
        y2, x2 = y + even * (1 - 2 * y), x + odd * (1 - 2 * x)
        return (y1, x1), (y2, x2)

    def attn_arrived(origin):
        o, there = origin()
        (y1, x1), (y2, x2) = neighbours(o)
        for n, ref in enumerate((qkv_at(r, o), wo_at(r, o))):
            links.put(ref, ref, s_first[n] + o, s_first[n] + o, place(y1, x1, c, z), there)
            links.put(ref, ref, s_own[n] + o, s_own[n] + o, place(y2, x2, c, z), there)

    def attn_forward(o, there):
        (y1, x1), (y2, x2) = neighbours(o)
        r1 = 2 * y1 + x1
        for n, ref in enumerate((qkv_at(r1, o), wo_at(r1, o))):
            def arrive(n=n, ref=ref):
                links.wait(ref, s_first[n] + o, to_x)

            arrive() if there is None else pl.when(there)(arrive)

            links.put(ref, ref, s_fwd[n] + o, s_fwd[n] + o, place(y2, x2, c, z), there)

    def attn_finish():
        for o in range(4):
            (y1, x1), (y2, x2) = neighbours(o)
            for n, at in enumerate((qkv_at, wo_at)):
                links.wait(at(2 * y2 + x2, o), s_own[n] + o, to_x)
                links.wait(at(2 * (1 - y) + 1 - x, o), s_fwd[n] + o, to_x)

    attn_line = Line("attn", lambda o: (qkv_at(r, o), wo_at(r, o)), attn_arrived)
    up_at = lambda yy, o: up.at[at_rows(yy * 512, 512, 512), at_rows(o * 256, 256, 256)]
    down_at = lambda yy, o: down.at[at_rows(o * 256, 256, 256), at_rows(yy * 512, 512, 512)]
    s_upy, s_downy = links.base("upy", 4), links.base("downy", 4)

    def across(at, base):
        def arrived(origin):
            def make():
                o, there = origin()
                return at(y, o), at(y, o), base + o, base + o, to_y, there

            links.start(make)

        return arrived

    up_line = Line("upl", lambda o: (up_at(y, o),), across(up_at, s_upy))
    down_line = Line("downl", lambda o: (down_at(y, o),), across(down_at, s_downy))

    lse[...] = jnp.zeros_like(lse)
    own_qkv.wait()
    own_wo.wait()
    links.wait(qkv_other, s_pc, to_c)
    links.wait(wo_other, s_pc + 1, to_c)
    attn_line.begin()
    for one in own_small:
        one.wait()
    for dd in range(1, 8):
        source = 4 * ((y + dd // 4) % 2) + 2 * ((x + (dd // 2) % 2) % 2) + (c + dd % 2) % 2
        links.wait(norm.at[source], s_norm + dd, to_c)
    for dz in range(1, 4):
        links.wait(bias.at[(z + 4 - dz) % 4], s_bias + dz, to_c)
    links.wait(mask.at[1 - c], s_mask, to_c)
    for dd in range(8):
        norm_row[:, dd * 128 : dd * 128 + 128] = norm[dd]
    for zz in range(4):
        qkv_row[:, zz * 384 : zz * 384 + 128] = bias[zz, 0:1]
        qkv_row[:, zz * 384 + 128 : zz * 384 + 256] = jnp.zeros((1, 128), F32)
        qkv_row[:, zz * 384 + 256 : zz * 384 + 384] = bias[zz, 1:2]
        up_row[:, zz * 256 : zz * 256 + 128] = bias[zz, 2:3]
        up_row[:, zz * 256 + 128 : zz * 256 + 256] = bias[zz, 3:4]

    own_up.wait()
    own_down.wait()
    attn_line.step(1)
    attn_forward(z, None)

    wait_tokens("tok", tok_in, lambda cc: tok, 5)

    @pl.loop(0, HALF // 32)
    def _(i):
        v = tok[at_rows(i * 32, 32, 32), :].astype(F32)
        unit, _ = unit_rows(v)
        n1[at_rows(c * HALF + i * 32, 32, 32), :] = (unit * norm_row[0:1] + norm_row[2:3]).astype(BF)

    s_n1 = links.base("n1", 1)
    half_at = lambda ref, cc: ref.at[at_rows(cc * HALF, HALF, 64), :]
    links.put(half_at(n1, c), half_at(n1, c), s_n1, s_n1, to_c)

    def forward_far(far):
        attn_forward(jnp.clip(z - far, 0, 3), z >= far)
        attn_forward(jnp.clip(z + far, 0, 3), z + far < 4)

    attn_line.step(2)
    forward_far(1)
    attn_line.step(3)
    for dx, dc in ((1, 0), (1, 1), (0, 1)):
        rel, sx, sc = 2 * dx + dc, (x + dx) % 2, (c + dc) % 2
        links.wait(up_shard(sx, sc), s_up + rel, to_c)
    up_line.begin()
    forward_far(2)
    move_tokens("cot", cot_in, lambda cc: block_at(cot, 2 * x + cc), 8)
    for dx, dc in ((1, 0), (1, 1), (0, 1)):
        rel, sx, sc = 2 * dx + dc, (x + dx) % 2, (c + dc) % 2
        links.wait(down_shard(sx, sc), s_down + rel, to_c)
    up_line.step(1)
    forward_far(3)
    down_line.begin()
    links.wait(half_at(n1, 1 - c), s_n1, to_c)
    attn_finish()

    @pl.loop(0, 6)
    def _(j):
        columns = at_rows(j * 256, 256, 256)
        proj[:, columns] = (mm(n1[...], qkv[:, columns], NN) + qkv_row[:, columns]).astype(BF)

    lane = lax.broadcasted_iota(jnp.int32, (1, 128), 1)
    first_head = lane < 64
    zero = jnp.zeros((), BF)
    up_line.step(2)

    @pl.loop(0, 4)
    def _(zz):
        keys = proj[:, at_rows(zz * 384 + 128, 128, 128)]
        values = proj[:, at_rows(zz * 384 + 256, 128, 128)]
        hidden_key = mask[z // 2, z % 2]
        for rb in range(2):
            rows = pl.ds(rb * HALF, HALF)
            pair = proj[rows, at_rows(zz * 384, 128, 128)]
            outs = []
            for hh in range(2):
                own = jnp.where(first_head if hh == 0 else jnp.logical_not(first_head), pair, zero)
                scores = mm(own, keys, NT) * (HD ** (-0.5)) + hidden_key
                highest = jnp.max(scores, axis=-1, keepdims=True)
                exponent = jnp.exp(scores - highest)
                total = jnp.sum(exponent, axis=-1, keepdims=True)
                low = (exponent * (1.0 / total)).astype(BF)
                head = 2 * zz + hh
                lse[rows, :] = jnp.where(lane == head, highest + jnp.log(total), lse[rows, :])
                outs.append(mm(low, values, NN))
            mix[rows, at_rows(zz * 128, 128, 128)] = jnp.where(first_head, outs[0], outs[1]).astype(BF)

        @pl.when(zz == 0)
        def _():
            down_line.step(1)

        @pl.when(zz == 1)
        def _():
            up_line.step(3)

        @pl.when(zz == 2)
        def _():
            down_line.step(2)

    down_line.step(3)

    s_part = links.base("part", 1)

    def project_out(cc, target):
        @pl.loop(0, 4)
        def _(j):
            columns = at_rows(j * 256, 256, 256)
            target[:, columns] = mm(mix[at_rows(cc * HALF, HALF, 64), :], wo[:, columns], NN)

    project_out(1 - c, part)
    links.put(part, got_part, s_part, s_part, to_c)
    project_out(c, hid)
    links.wait(got_part, s_part, to_c)

    @pl.loop(0, HALF // 32)
    def _(i):
        rows = at_rows(i * 32, 32, 32)
        v = hid[rows, :] + got_part[rows, :] + tok[rows, :].astype(F32) + norm_row[4:5]
        hid[rows, :] = v
        unit, _ = unit_rows(v)
        n2[block_rows(q, i * 32, 32), :] = (unit * norm_row[1:2] + norm_row[3:4]).astype(BF)

    def spread_start(key, ref):
        base = links.base(("spread", key), 3)
        links.put(block_at(ref, q), block_at(ref, q), base, base, to_x)
        links.put(block_at(ref, q), block_at(ref, q), base + 1, base + 1, to_c)

    def spread_forward(key, ref):
        base = links.base(("spread", key), 3)
        far = block_at(ref, 2 * (1 - x) + c)
        links.wait(far, base, to_x)
        links.put(far, far, base + 2, base + 2, to_c)

    def spread_wait_near(key, ref):
        links.wait(block_at(ref, 2 * x + 1 - c), links.base(("spread", key), 3) + 1, to_c)

    def spread_wait_far(key, ref):
        links.wait(block_at(ref, 2 * (1 - x) + 1 - c), links.base(("spread", key), 3) + 2, to_c)

    spread_start("n2", n2)
    wait_tokens("cot", cot_in, lambda cc: block_at(cot, 2 * x + cc), 8)
    spread_start("cot", cot)
    for o in range(4):
        links.wait(up_at(1 - y, o), s_upy + o, to_y)

    def expand(t):
        @pl.loop(0, 4)
        def _(j):
            columns = at_rows(j * 256, 256, 256)
            for rb in range(2):
                rows = block_rows(t, rb * Q, Q)
                v = mm(n2[rows, :], up[:, columns], NN) + up_row[:, columns]
                value, grade = gelu_both(v)
                act[rows, columns] = value.astype(BF)
                slope[rows, columns] = grade.astype(BF)

    expand(q)
    spread_wait_near("n2", n2)
    expand(2 * x + 1 - c)
    spread_forward("n2", n2)
    expand(2 * (1 - x) + c)
    spread_wait_far("n2", n2)
    expand(2 * (1 - x) + 1 - c)
    spread_wait_near("cot", cot)
    spread_forward("cot", cot)
    spread_wait_far("cot", cot)
    for o in range(4):
        links.wait(down_at(1 - y, o), s_downy + o, to_y)

    near_other, far_own, far_other = 2 * x + 1 - c, 2 * (1 - x) + c, 2 * (1 - x) + 1 - c
    sums[...] = jnp.zeros_like(sums)
    gb1[...] = jnp.zeros_like(gb1)

    def fold(v):
        return v[0:8] + v[8:16] + v[16:24] + v[24:32]

    def tally(row, v):
        sums[row * 8 : row * 8 + 8, :] += fold(v)

    def send_later(make):
        links.start(make)

    def through_slope(t):
        @pl.loop(0, 4)
        def _(j):
            columns = at_rows(j * 256, 256, 256)
            rows = block_rows(t, 0, HALF)
            v = mm(cot[rows, :], down[columns, :], NT) * slope[rows, columns].astype(F32)
            gb1[:, columns] += jnp.sum(v.reshape(HALF // 8, 8, 256), axis=0)
            slope[rows, columns] = v.astype(BF)

    def back_part(t, target):
        @pl.loop(0, 4)
        def _(j):
            columns = at_rows(j * 256, 256, 256)
            target[:, columns] = mm(slope[block_rows(t, 0, HALF), :], up[columns, :], NT).astype(target.dtype)

    def add_rows(target, *sources):
        @pl.loop(0, HALF // 32)
        def _(i):
            rows = at_rows(i * 32, 32, 32)
            total = sources[0][rows, :].astype(F32)
            for source in sources[1:]:
                total = total + source[rows, :].astype(F32)
            target[rows, :] = total.astype(target.dtype)

    s_gfar, s_gmid, s_gnear = links.base("gfar", 1), links.base("gmid", 1), links.base("gnear", 1)
    s_bfar, s_bmid, s_bnear = links.base("bfar", 1), links.base("bmid", 1), links.base("bnear", 1)
    through_slope(far_other)
    back_part(far_other, s_far)
    links.put(s_far, g_far, s_gfar, s_gfar, to_c)
    through_slope(far_own)
    links.copy(part, got_part, s_part, s_part, to_c).wait_send()
    links.drop(s_part)
    back_part(far_own, part)
    links.wait(g_far, s_gfar, to_c)
    add_rows(s_mid, part, g_far)
    links.put(s_mid, g_mid, s_gmid, s_gmid, to_x)
    through_slope(near_other)
    back_part(near_other, s_near)
    links.put(s_near, g_near, s_gnear, s_gnear, to_c)
    through_slope(q)
    back_part(q, part)

    s_rdown, s_rup = links.base("rdown", 4), links.base("rup", 4)
    d_down_at = lambda yy, o: d_down.at[at_rows(o * 256, 256, 256), at_rows(yy * 512, 512, 512)]
    d_up_at = lambda yy, o: d_up.at[at_rows(yy * 512, 512, 512), at_rows(o * 256, 256, 256)]
    r_down_at = lambda o: r_down.at[at_rows(o * 256, 256, 256), :]
    r_up_at = lambda o: r_up.at[:, at_rows(o * 256, 256, 256)]

    def make_rdown(k):
        o = (z + 1 + k) % 4
        return d_down_at(1 - y, o), r_down_at(o), s_rdown + o, s_rdown + o, to_y, None

    def make_rup(k):
        o = (z + 1 + k) % 4
        return d_up_at(1 - y, o), r_up_at(o), s_rup + o, s_rup + o, to_y, None

    for k in range(4):
        rows = at_rows(((z + 1 + k) % 4) * 256, 256, 256)
        d_down[rows, :] = mm(act[:, rows], cot[...], TN).astype(BF)
        links.start(functools.partial(make_rdown, k))
    for k in range(4):
        columns = at_rows(((z + 1 + k) % 4) * 256, 256, 256)
        d_up[:, columns] = mm(n2[...], slope[:, columns], TN).astype(BF)
        links.start(functools.partial(make_rup, k))

    links.wait(g_near, s_gnear, to_c)
    links.wait(g_mid, s_gmid, to_x)

    @pl.loop(0, HALF // 32)
    def _(i):
        rows = at_rows(i * 32, 32, 32)
        grad = part[rows, :] + g_near[rows, :].astype(F32) + g_mid[rows, :].astype(F32)
        unit, scale = unit_rows(hid[rows, :])
        out = cot[block_rows(q, i * 32, 32), :].astype(F32)
        scaled = grad * norm_row[1:2]
        moved = scale * (
            scaled
            - jnp.mean(scaled, axis=-1, keepdims=True)
            - unit * jnp.mean(scaled * unit, axis=-1, keepdims=True)
        )
        total = out + moved
        tally(1, grad * unit)
        tally(3, grad)
        tally(4, total)
        tally(5, out)
        got_part[rows, :] = total
        ga[at_rows(c * HALF + i * 32, 32, 32), :] = total.astype(BF)

    s_ga = links.base("ga", 1)
    links.put(half_at(ga, c), half_at(ga, c), s_ga, s_ga, to_c)

    def down_part(t, target, base=None):
        @pl.loop(0, 4)
        def _(j):
            columns = at_rows(j * 256, 256, 256)
            v = mm(act[block_rows(t, 0, HALF), :], down[:, columns], NN)
            target[:, columns] = (v if base is None else v + base[:, columns]).astype(target.dtype)

    links.copy(s_far, g_far, s_gfar, s_gfar, to_c).wait_send()
    links.copy(s_mid, g_mid, s_gmid, s_gmid, to_x).wait_send()
    links.copy(s_near, g_near, s_gnear, s_gnear, to_c).wait_send()
    links.drop(s_gfar, s_gmid, s_gnear)
    down_part(far_other, s_far)
    links.put(s_far, b_far, s_bfar, s_bfar, to_c)

    links.wait(half_at(ga, 1 - c), s_ga, to_c)

    @pl.loop(0, 2)
    def _(j):
        columns = at_rows(j * 256, 256, 256)
        gmix[:, columns] = mm(ga[...], wo[columns, :], NT).astype(BF)

    @pl.loop(0, 2)
    def _(j):
        columns = at_rows(j * 256, 256, 256)
        d_wo[columns, :] = mm(mix[:, columns], ga[...], TN).astype(BF)

    d_qkv_at = lambda rr, o: d_qkv.at[at_rows(rr * 256, 256, 256), at_rows(o * 384, 384, 128)]
    d_wo_at = lambda rr, o: d_wo.at[at_rows(o * 128, 128, 128), at_rows(rr * 256, 256, 128)]

    def accumulate(target, *sources):
        count = target.shape[0] // 64

        @pl.loop(0, count)
        def _(i):
            rows = at_rows(i * 64, 64, 64)
            total = target[rows, :].astype(F32)
            for source in sources:
                total = total + source[rows, :].astype(F32)
            target[rows, :] = total.astype(target.dtype)

    class Reduce:
        def __init__(self, key, at, first, second, over_z, final):
            self.at, self.first, self.second, self.over_z, self.final = at, first, second, over_z, final
            self.s1 = [links.base((key, "first", i), 4) for i in range(2)]
            self.s2, self.sz = links.base((key, "second"), 4), links.base((key, "z"), 8)

        def begin(self, o):
            def make(i):
                (y1, x1), (y2, x2) = neighbours(o)
                rr = 2 * y1 + x1 if i == 0 else 3 - r
                return self.at(rr, o), self.first.at[i, o], self.s1[i] + o, self.s1[i] + o, place(y1, x1, c, z), None

            for i in (1, 0):
                links.start(functools.partial(make, i))

        def middle(self, o):
            (y1, x1), (y2, x2) = neighbours(o)
            links.wait(self.first.at[1, o], self.s1[1] + o, to_x)
            accumulate(self.at(2 * y2 + x2, o), self.first.at[1, o])

            def make():
                (y1, x1), (y2, x2) = neighbours(o)
                return self.at(2 * y2 + x2, o), self.second.at[o], self.s2 + o, self.s2 + o, place(y2, x2, c, z), None

            links.start(make)

        def gather(self, k):
            o = (z + 1 + k) % 4
            links.wait(self.first.at[0, o], self.s1[0] + o, to_x)
            links.wait(self.second.at[o], self.s2 + o, to_x)
            accumulate(self.at(r, o), self.first.at[0, o], self.second.at[o])
            if k < 3:
                push_z(self, k, lambda o: self.at(r, o))

        def last(self):
            finish_z(self, self.at(r, z))

    def push_z(owner, k, at):
        def make():
            o = (z + 1 + k) % 4
            return at(o), owner.over_z.at[z], owner.sz + k, owner.sz + 4 + z, place(y, x, c, o), None

        links.start(make)

    def finish_z(owner, own):
        for k in range(3):
            source = (z + 1 + k) % 4
            links.wait(owner.over_z.at[source], owner.sz + 4 + source, up_z_other)
        others = [owner.over_z.at[(z + 1 + k) % 4] for k in range(3)]
        count = own.shape[0] // 64

        @pl.loop(0, count)
        def _(i):
            rows = at_rows(i * 64, 64, 64)
            total = own[rows, :].astype(F32)
            for other in others:
                total = total + other[rows, :].astype(F32)
            owner.final[rows, :] = total.astype(BF)

    up_z_other = to_c
    red_wo = Reduce("red_wo", d_wo_at, first_wo, second_wo, z_wo, f_wo)
    red_qkv = Reduce("red_qkv", d_qkv_at, first_qkv, second_qkv, z_qkv, f_qkv)
    for o in range(4):
        red_wo.begin(o)

    class Half:
        def __init__(self, key, at, got_at, s_got, over_z, final):
            self.at, self.got_at, self.s_got, self.over_z, self.final = at, got_at, s_got, over_z, final
            self.sz = links.base((key, "z"), 8)

        def gather(self, k):
            o = (z + 1 + k) % 4
            links.wait(self.got_at(o), self.s_got + o, to_y)
            accumulate(self.at(y, o), self.got_at(o))
            if k < 3:
                push_z(self, k, lambda o: self.at(y, o))

        def last(self):
            finish_z(self, self.at(y, z))

    half_down = Half("half_down", d_down_at, r_down_at, s_rdown, z_down, f_down)
    half_up = Half("half_up", d_up_at, r_up_at, s_rup, z_up, f_up)

    down_part(far_own, part)
    links.wait(b_far, s_bfar, to_c)
    add_rows(s_mid, part, b_far)
    links.put(s_mid, b_mid, s_bmid, s_bmid, to_x)
    down_part(near_other, s_near)
    links.put(s_near, b_near, s_bnear, s_bnear, to_c)
    down_part(q, hid, hid)

    @pl.loop(0, 4)
    def _(zz):
        base = zz * 384
        keys = proj[:, at_rows(base + 128, 128, 128)]
        values = proj[:, at_rows(base + 256, 128, 128)]
        hidden_key = mask[z // 2, z % 2]
        d_keys = d_values = None
        sum_queries = None
        for rb in range(2):
            rows = pl.ds(rb * HALF, HALF)
            pair = proj[rows, at_rows(base, 128, 128)]
            grads = gmix[rows, at_rows(zz * 128, 128, 128)]
            outs = []
            for hh in range(2):
                keep = first_head if hh == 0 else jnp.logical_not(first_head)
                own = jnp.where(keep, pair, zero)
                own_grad = jnp.where(keep, grads, zero)
                level = jnp.sum(jnp.where(lane == 2 * zz + hh, lse[rows, :], 0.0), axis=-1, keepdims=True)
                attention = jnp.exp(mm(own, keys, NT) * (HD ** (-0.5)) + hidden_key - level)
                grad_attention = mm(own_grad, values, NT)
                inner = jnp.sum(attention * grad_attention, axis=-1, keepdims=True)
                low = (attention * (grad_attention - inner)).astype(BF)
                more_values = mm(attention.astype(BF), own_grad, TN)
                more_keys = mm(low, own, TN)
                d_values = more_values if d_values is None else d_values + more_values
                d_keys = more_keys if d_keys is None else d_keys + more_keys
                outs.append(mm(low, keys, NN))
            d_queries = jnp.where(first_head, outs[0], outs[1]) * (HD ** (-0.5))
            total = jnp.sum(d_queries.reshape(HALF // 8, 8, 128), axis=0)
            sum_queries = total if sum_queries is None else sum_queries + total
            gproj[rows, at_rows(base, 128, 128)] = d_queries.astype(BF)
        gproj[:, at_rows(base + 128, 128, 128)] = (d_keys * (HD ** (-0.5))).astype(BF)
        gproj[:, at_rows(base + 256, 128, 128)] = d_values.astype(BF)
        gbq[:, at_rows(zz * 128, 128, 128)] = sum_queries
        gbv[:, at_rows(zz * 128, 128, 128)] = jnp.sum(d_values.reshape(FULL // 8, 8, 128), axis=0)

        @pl.when(zz == 0)
        def _():
            for o in range(4):
                red_wo.middle(o)

        @pl.when(zz == 1)
        def _():
            for k in range(4):
                half_down.gather(k)

        @pl.when(zz == 2)
        def _():
            for k in range(4):
                half_up.gather(k)

    links.wait(b_near, s_bnear, to_c)
    links.wait(b_mid, s_bmid, to_x)
    links.copy(s_far, b_far, s_bfar, s_bfar, to_c).wait_send()
    links.copy(s_near, b_near, s_bnear, s_bnear, to_c).wait_send()
    links.drop(s_bfar, s_bnear)

    @pl.loop(0, HALF // 32)
    def _(i):
        rows = at_rows(i * 32, 32, 32)
        total = hid[rows, :] + b_near[rows, :].astype(F32) + b_mid[rows, :].astype(F32) + norm_row[5:6]
        s_near[rows, :] = total.astype(BF)

    def send_home(key, source, target, at):
        base = links.base(key, 4)
        for j in range(2):
            def make(j=j):
                here = jnp.logical_and(z // 2 == c, z == 2 * c + j)
                to = place(y, x, z // 2, 2 * c + j)
                to = (jnp.where(here, place(y, x, 1 - c, z)[0], to[0]), to[1])
                return source.at[pl.ds(j * Q, Q)], target.at[z % 2], base + j, base + 2 + z % 2, to, jnp.logical_not(here)

            links.start(make)

            @pl.when(jnp.logical_and(z // 2 == c, z == 2 * c + j))
            def _(j=j):
                local(at, source.at[pl.ds(j * Q, Q)], target.at[z % 2]).start()

    def wait_home(key, source, target, at):
        base = links.base(key, 4)
        for i in range(2):
            here = jnp.logical_and(z // 2 == c, z % 2 == i)

            @pl.when(here)
            def _(i=i):
                local(at, source.at[pl.ds(0, Q)], target.at[i]).wait()

            @pl.when(jnp.logical_not(here))
            def _(i=i):
                links.wait(target.at[i], base + 2 + i, to_c)

    send_home("block", s_near, block_out, 9)

    def weigh(rr):
        d_qkv[at_rows(rr * 256, 256, 256), :] = mm(n1[:, at_rows(rr * 256, 256, 256)], gproj[...], TN).astype(BF)

    weigh(3 - r)
    weigh(2 * y + 1 - x)
    red_qkv.begin(0)
    red_qkv.begin(2)
    weigh(2 * (1 - y) + x)
    red_qkv.begin(1)
    red_qkv.begin(3)

    def front_part(cc, target):
        @pl.loop(0, 4)
        def _(j):
            columns = at_rows(j * 256, 256, 256)
            target[:, columns] = mm(gproj[at_rows(cc * HALF, HALF, 64), :], qkv[columns, :], NT).astype(target.dtype)

    s_gn1 = links.base("gn1", 1)
    front_part(1 - c, s_far)
    links.put(s_far, g_n1, s_gn1, s_gn1, to_c)
    weigh(r)
    front_part(c, part)
    links.wait(g_n1, s_gn1, to_c)
    links.copy(s_mid, b_mid, s_bmid, s_bmid, to_x).wait_send()
    links.drop(s_bmid)

    @pl.loop(0, HALF // 32)
    def _(i):
        rows = at_rows(i * 32, 32, 32)
        grad = part[rows, :] + g_n1[rows, :].astype(F32)
        unit, scale = unit_rows(tok[rows, :].astype(F32))
        scaled = grad * norm_row[0:1]
        moved = scale * (
            scaled
            - jnp.mean(scaled, axis=-1, keepdims=True)
            - unit * jnp.mean(scaled * unit, axis=-1, keepdims=True)
        )
        tally(0, grad * unit)
        tally(2, grad)
        s_mid[rows, :] = (got_part[rows, :] + moved).astype(BF)

    send_home("home", s_mid, grad_out, 10)

    for row in range(6):
        sums_row[row : row + 1, :] = jnp.sum(sums[row * 8 : row * 8 + 8, :], axis=0, keepdims=True)
    sums_row[6:8, :] = jnp.zeros((2, 1024), F32)
    for dd in range(8):
        norm[dd] = sums_row[:, dd * 128 : dd * 128 + 128]
    s_sum, s_sumz = links.base("sum", 8), links.base("sumz", 8)
    for dd in range(1, 8):
        def make(dd=dd):
            ty, tx, tc = (y + dd // 4) % 2, (x + (dd // 2) % 2) % 2, (c + dd % 2) % 2
            return norm.at[4 * ty + 2 * tx + tc], sums_got.at[dd], s_sum + dd, s_sum + dd, place(ty, tx, tc, z), None

        links.start(make)
    for zz in range(4):
        flat = lambda ref, start: jnp.sum(ref[:, start : start + 128], axis=0, keepdims=True)
        bias_pack[zz, 0:1] = flat(gbq, zz * 128)
        bias_pack[zz, 1:2] = flat(gbv, zz * 128)
        bias_pack[zz, 2:3] = flat(gb1, zz * 256)
        bias_pack[zz, 3:4] = flat(gb1, zz * 256 + 128)
        bias_pack[zz, 4:8] = jnp.zeros((4, 128), F32)
    s_bz, s_ball = links.base("bz", 4), links.base("ball", 8)
    for dz in range(1, 4):
        def make(dz=dz):
            tz = (z + dz) % 4
            return bias_pack.at[tz], bias_got.at[dz], s_bz + dz, s_bz + dz, place(y, x, c, tz), None

        links.start(make)

    for o in range(4):
        red_qkv.middle(o)
    for k in range(4):
        red_wo.gather(k)

    for dz in range(1, 4):
        links.wait(bias_got.at[dz], s_bz + dz, to_c)
    bias_all[d] = bias_pack[z] + bias_got[1] + bias_got[2] + bias_got[3]
    for dd in range(1, 8):
        def make(dd=dd):
            to = place((y + dd // 4) % 2, (x + (dd // 2) % 2) % 2, (c + dd % 2) % 2, z)
            return bias_all.at[d], bias_all.at[d], s_ball + dd, s_ball + dd, to, None

        links.start(make)
    for dd in range(1, 8):
        links.wait(sums_got.at[dd], s_sum + dd, to_c)
    total = norm[d]
    for dd in range(1, 8):
        total = total + sums_got[dd]
    sums_z[0] = total
    for dz in range(1, 4):
        def make(dz=dz):
            return sums_z.at[0], sums_z.at[dz], s_sumz + dz, s_sumz + dz, place(y, x, c, (z + dz) % 4), None

        links.start(make)

    half_down.last()
    half_up.last()
    s_oup, s_odown = links.base("oup", 4), links.base("odown", 4)
    for dx, dc in ((1, 0), (1, 1), (0, 1)):
        rel = 2 * dx + dc

        def make_up(dx=dx, dc=dc, rel=rel):
            tx, tc = (x + dx) % 2, (c + dc) % 2
            rows = at_rows((2 * tx + tc) * 128, 128, 128)
            return f_up.at[rows, :], o_up.at[q], s_oup + rel, s_oup + rel, place(y, tx, tc, z), None

        def make_down(dx=dx, dc=dc, rel=rel):
            tx, tc = (x + dx) % 2, (c + dc) % 2
            columns = at_rows((2 * tx + tc) * 128, 128, 128)
            return f_down.at[:, columns], o_down.at[q], s_odown + rel, s_odown + rel, place(y, tx, tc, z), None

        links.start(make_up)
        links.start(make_down)

    for k in range(4):
        red_qkv.gather(k)
    red_wo.last()

    w1_out[:, at_rows(q * 256, 256, 256)] = f_up[at_rows(q * 128, 128, 128), :].astype(F32)
    w2_out[at_rows(q * 256, 256, 256), :] = f_down[:, at_rows(q * 128, 128, 128)].astype(F32)
    for dx, dc in ((1, 0), (1, 1), (0, 1)):
        rel, source = 2 * dx + dc, 2 * ((x + dx) % 2) + (c + dc) % 2
        links.wait(o_up.at[source], s_oup + rel, to_c)
        links.wait(o_down.at[source], s_odown + rel, to_c)
        w1_out[:, at_rows(source * 256, 256, 256)] = o_up[source].astype(F32)
        w2_out[at_rows(source * 256, 256, 256), :] = o_down[source].astype(F32)

    for dd in range(1, 8):
        source = 4 * ((y + dd // 4) % 2) + 2 * ((x + (dd // 2) % 2) % 2) + (c + dd % 2) % 2
        links.wait(bias_all.at[source], s_ball + dd, to_c)
    for cc in range(2):
        together = bias_all[cc] + bias_all[2 + cc] + bias_all[4 + cc] + bias_all[6 + cc]
        qv_out[:, cc * 128 : cc * 128 + 128] = together[0:2]
    for qq in range(4):
        together = bias_all[qq] + bias_all[4 + qq]
        b1_out[qq * 2 : qq * 2 + 2, :] = together[2:4]
    for dz in range(1, 4):
        links.wait(sums_z.at[dz], s_sumz + dz, to_c)
    sums_out[...] = sums_z[0] + sums_z[1] + sums_z[2] + sums_z[3]

    red_qkv.last()
    s_oqkv, s_owo = links.base("oqkv", 1), links.base("owo", 1)
    links.put(f_qkv.at[at_rows((1 - c) * 128, 128, 128), :], o_qkv, s_oqkv, s_oqkv, to_c)
    links.put(f_wo.at[:, at_rows((1 - c) * 128, 128, 128)], o_wo, s_owo, s_owo, to_c)
    qkv_out[:, at_rows(c * 384, 384, 128)] = f_qkv[at_rows(c * 128, 128, 128), :].astype(F32)
    wo_out[at_rows(c * 128, 128, 128), :] = f_wo[:, at_rows(c * 128, 128, 128)].astype(F32)
    links.wait(o_qkv, s_oqkv, to_c)
    links.wait(o_wo, s_owo, to_c)
    qkv_out[:, at_rows((1 - c) * 384, 384, 128)] = o_qkv[...].astype(F32)
    wo_out[at_rows((1 - c) * 128, 128, 128), :] = o_wo[...].astype(F32)
    wait_home("block", s_near, block_out, 9)
    wait_home("home", s_mid, grad_out, 10)
    links.finish()


def prepare(inputs, valid_mask, cotangent, ln_gain, d_bias, w_qkv, b_qv, b_1):
    y, x, c, z = where_am_i()
    rows = inputs.shape[0]
    turn = lambda v: jnp.pad(jnp.transpose(v, (1, 0, 2)), ((0, 0), (0, Q - rows), (0, 0)))
    mask = jnp.where(valid_mask.reshape(2, 4, rows) > 0, 0.0, MASKED).astype(F32)
    mask = jnp.pad(mask, ((0, 0), (0, 0), (0, Q - rows)), constant_values=MASKED).reshape(2, 1, FULL)
    norm = jnp.pad(jnp.concatenate([ln_gain, d_bias]).astype(F32), ((0, 2), (0, 0)))
    bias = jnp.concatenate(
        [
            lax.dynamic_slice(b_qv, (0, c * 128), (2, 128)),
            lax.dynamic_slice(b_1, ((2 * x + c) * 256,), (256,)).reshape(2, 128),
        ]
    ).astype(F32)
    bias = jnp.pad(bias, ((0, 4), (0, 0)))
    qkv = jnp.transpose(w_qkv.reshape(128, 3, 2, 128), (0, 2, 1, 3)).reshape(128, 768)
    return turn(inputs), turn(cotangent), mask, norm, bias, qkv


def layer_call(*operands):
    shape = jax.ShapeDtypeStruct
    hbm, vmem = pl.BlockSpec(memory_space=pl.ANY), pl.BlockSpec(memory_space=pltpu.VMEM)
    outs = [
        shape((2, Q, 1024), BF), shape((2, Q, 1024), BF), shape((8, 128), F32), shape((2, 256), F32),
        shape((8, 128), F32), shape((128, 768), F32), shape((256, 128), F32), shape((128, 1024), F32),
        shape((1024, 128), F32),
    ]
    low = lambda *dims: pltpu.VMEM(dims, BF)
    wide = lambda *dims: pltpu.VMEM(dims, F32)
    scratch = [
        low(HALF, 1024), low(4 * HALF, 1024), wide(2, 2, 1, FULL), wide(8, 8, 128), wide(4, 8, 128),
        low(1024, 1536), low(512, 1024), low(1024, 1024), low(1024, 1024),
        low(FULL, 1024), low(FULL, 1536), wide(FULL, 128), low(FULL, 512), wide(HALF, 1024),
        low(4 * HALF, 1024), low(4 * HALF, 1024), low(4 * HALF, 1024),
        wide(8, 1024), wide(1, 1536), wide(1, 1024), wide(HALF, 1024), wide(HALF, 1024),
        low(FULL, 1024), low(FULL, 512), low(FULL, 1536),
        low(1024, 1024), low(1024, 1024), low(1024, 1536), low(512, 1024),
        low(512, 1024), low(1024, 512), low(4, 512, 256), low(4, 256, 512),
        low(512, 256), low(256, 512), low(4, 128, 256), low(4, 256, 128),
        low(2, 4, 256, 384), low(2, 4, 128, 256), low(4, 256, 384), low(4, 128, 256),
        low(4, 256, 384), low(4, 128, 256), low(256, 384), low(128, 256), low(128, 384), low(128, 128),
        *[low(HALF, 1024)] * 10,
        wide(48, 1024), wide(8, 1024), wide(8, 8, 128), wide(4, 8, 128),
        wide(8, 1024), wide(8, 512), wide(8, 512), wide(4, 8, 128), wide(4, 8, 128), wide(8, 8, 128),
        pltpu.SemaphoreType.DMA((16,)), pltpu.SemaphoreType.DMA((320,)), pltpu.SemaphoreType.DMA((320,)),
    ]
    return pl.pallas_call(
        layer_kernel,
        out_shape=outs,
        in_specs=[hbm] * 9,
        out_specs=[hbm, hbm] + [vmem] * 7,
        scratch_shapes=scratch,
        compiler_params=pltpu.CompilerParams(collective_id=0, has_side_effects=True, vmem_limit_bytes=67043328),
        name="layer",
    )(*operands)


def fast_body(inputs, valid_mask, cotangent, ln_gain, d_bias, w_qkv, b_qv, w_o, w_1, b_1, w_2):
    rows = inputs.shape[0]
    block, grad, sums, qv, b1, qkv, wo, w1, w2 = layer_call(
        *prepare(inputs, valid_mask, cotangent, ln_gain, d_bias, w_qkv, b_qv, b_1), w_o, w_1, w_2
    )
    back = lambda v: jnp.transpose(v[:, :rows], (1, 0, 2))
    w_qkv_grad = jnp.transpose(qkv.reshape(128, 2, 3, 128), (0, 2, 1, 3)).reshape(128, 3, 256)
    return (
        back(block), back(grad).astype(F32), sums[:2], sums[2:6], w_qkv_grad, qv, wo, w1, b1.reshape(1024), w2,
    )


def solution(mesh):
    in_specs = (
        P("tensor", "dp", None),
        P("dp", None),
        P("tensor", "dp", None),
        P(None, "dp"),
        P(None, "dp"),
        P("dp", None, "tensor"),
        P(None, "tensor"),
        P("tensor", "dp"),
        P("dp", "tensor"),
        P("tensor"),
        P("tensor", "dp"),
    )
    out_specs = (
        P("tensor", "dp", None),
        P("tensor", "dp", None),
        P(None, "dp"),
        P(None, "dp"),
        P("dp", None, "tensor"),
        P(None, "tensor"),
        P("tensor", "dp"),
        P("dp", "tensor"),
        P("tensor"),
        P("tensor", "dp"),
    )
    run = fast_body if dict(mesh.shape) == {"dp": 8, "tensor": 4} else body
    return jax.shard_map(run, mesh=mesh, in_specs=in_specs, out_specs=out_specs, check_vma=False)
```

profile of v0, /device:TPU:1, one launch (start us, length us, event | category | flops | bytes accessed | tf_op | source)
XLA Modules:
  0.0 308.1 jit_solution(1511188535376128239)
XLA Ops:
  0.6 0.0 copy-start
  0.7 0.8 dynamic-slice_bitcast_fusion
  1.5 0.7 constant_dynamic-slice_fusion
  2.2 0.6 fusion.7.bias_in
  2.8 1.3 fusion.5.norm_in
  4.0 0.7 compare_select_fusion
  4.7 0.1 select_n.29
  4.8 0.7 reshape.47.mask_in
  5.5 1.1 copy.35
  6.6 0.8 copy.37.qkv_in
  7.5 0.0 copy-done
  7.5 0.0 copy-start.1
  7.5 0.1 copy.46
  7.6 0.9 pad.23.tok_in
  8.5 0.0 copy-done.1
  8.5 0.1 copy.45
  8.7 0.9 pad.24.cot_in
  9.6 286.8 %layer.1 = (bf16[2,160,1024]{2,1,0:T(8,128)(2,1)}, bf16[2,160,1024]{2,1,0:T(8,128)(2,1)}, f32[8,128]{1,0:T(8,128)}, f32[2,256]{1,0:T(2,128)}, f32[8,128]{1,0:T(8...) custom-call(bf16[2,160,1024]{2,1,0:T(8,128)(2,1)} %pad.23.tok_in, ...), custom_call_target="tpu_custom_call" | custom-call | tf_op jit(solution)/shard_map/layer/pallas_call | solution.py:1245
  296.4 0.0 copy-start.2
  296.4 0.0 copy-start.3
  296.4 1.3 slice.14
  297.7 1.3 slice.15
  299.0 1.1 copy.38
  300.2 0.9 copy.42
  301.1 0.0 copy-done.2
  301.1 0.0 copy-done.3
  301.1 0.2 convert_bitcast_fusion
  301.3 0.0 copy-start.8
  301.3 0.0 copy-start.6
  301.3 1.9 copy.41
  303.2 0.0 copy-start.5
  303.2 0.0 copy-start.7
  303.2 0.0 copy-start.4
  303.2 1.4 copy.40
  304.7 0.0 copy-done.8
  304.7 0.6 copy.52
  305.2 0.0 copy-done.6
  305.2 0.7 copy.53
  305.9 0.0 copy-done.5
  305.9 0.8 copy.54
  306.7 0.0 copy-done.7
  306.7 0.6 copy.55
  307.3 0.0 copy-done.4
  307.3 0.8 copy.56
  (3 shorter events, 0.1 us)
Async XLA Ops:
  0.6 6.8 %copy-start = (bf16[146,2,1024]{2,1,0:T(2,128)(2,1)S(1)}, bf16[146,2,1024]{2,1,0:T(2,128)(2,1)}, u32[]{:S(2)}) copy-start(bf16[146,2,1024]{2,1,0:T(2,128)(2,1)} %param.11) | copy-start | bytes 1794052
  7.5 1.1 copy-start.1
  296.4 4.7 %copy-start.2 = (bf16[2,160,1024]{2,1,0:T(8,128)(2,1)S(1)}, bf16[2,160,1024]{2,1,0:T(8,128)(2,1)}, u32[]{:S(2)}) copy-start(bf16[2,160,1024]{2,1,0:T(8,128)(2,1)} %get-tuple-element.19) | copy-start | bytes 1966084
  296.4 4.7 %copy-start.3 = (bf16[2,160,1024]{2,1,0:T(8,128)(2,1)S(1)}, bf16[2,160,1024]{2,1,0:T(8,128)(2,1)}, u32[]{:S(2)}) copy-start(bf16[2,160,1024]{2,1,0:T(8,128)(2,1)} %get-tuple-element.20) | copy-start | bytes 1966084
  301.3 3.4 %copy-start.8 = (f32[2,256]{1,0:T(2,128)S(1)}, f32[2,256]{1,0:T(2,128)}, u32[]{:S(2)}) copy-start(f32[2,256]{1,0:T(2,128)} %get-tuple-element.75) | copy-start | bytes 6148
  301.3 4.0 %copy-start.6 = (f32[256,128]{1,0:T(8,128)S(1)}, f32[256,128]{1,0:T(8,128)}, u32[]{:S(2)}) copy-start(f32[256,128]{1,0:T(8,128)} %get-tuple-element.76) | copy-start | bytes 393220
  303.2 2.7 copy-start.5
  303.2 3.5 %copy-start.7 = (f32[8,128]{1,0:T(8,128)S(1)}, f32[8,128]{1,0:T(8,128)}, u32[]{:S(2)}) copy-start(f32[8,128]{1,0:T(8,128)} %get-tuple-element.26) | copy-start | bytes 12292
  303.2 4.1 %copy-start.4 = (f32[1024,128]{1,0:T(8,128)S(1)}, f32[1024,128]{1,0:T(8,128)}, u32[]{:S(2)}) copy-start(f32[1024,128]{1,0:T(8,128)} %get-tuple-element.79) | copy-start | bytes 1572868
where the time goes:
time: 311 us; the launch traced here: 308 us
  Pallas kernels  287 us (92%)
  local copies, waits for them, and re-layouts  17.8 us (6%)
    pallas_call x1, Pallas kernels, layer_call(): pl.pallas_call(layer_kernel, out_shape=outs, in_specs=[hbm] * 9, out_spec...  287 us
    unnamed x29, local copies, waits for them, and re-layouts  9.11 us

commit v1 on v0

--- a/solution.py
+++ b/solution.py
@@ -360,7 +360,6 @@
     links = Links(send_sem, recv_sem)
     me = place(y, x, c, z)
     to_c, to_x, to_y = place(y, x, 1 - c, z), place(y, 1 - x, c, z), place(1 - y, x, c, z)
-    up_z, down_z = place(y, x, c, jnp.minimum(z + 1, 3)), place(y, x, c, jnp.maximum(z - 1, 0))
     greet(y, x, c, z)
 
     block_at = lambda ref, t: ref.at[at_rows(t * HALF, HALF, 64), :]
@@ -369,22 +368,23 @@
     def local(at, src, dst):
         return pltpu.make_async_copy(src, dst, local_sem.at[at])
 
-    qkv_at = lambda rr, zz: qkv.at[at_rows(rr * 256, 256, 256), at_rows(zz * 384, 384, 128)]
-    wo_at = lambda rr, zz: wo.at[at_rows(zz * 128, 128, 128), at_rows(rr * 256, 256, 128)]
-    qkv_shard = qkv.at[at_rows(r * 256 + c * 128, 128, 128), at_rows(z * 384, 384, 128)]
-    wo_shard = wo.at[at_rows(z * 128, 128, 128), at_rows(r * 256 + c * 128, 128, 128)]
-    qkv_other = qkv.at[at_rows(r * 256 + (1 - c) * 128, 128, 128), at_rows(z * 384, 384, 128)]
-    wo_other = wo.at[at_rows(z * 128, 128, 128), at_rows(r * 256 + (1 - c) * 128, 128, 128)]
+    z1, z2, z3 = z + 1 - 2 * (z % 2), (z + 2) % 4, 3 - z
+    to_z1, to_z2 = place(y, x, c, z1), place(y, x, c, z2)
+    r_x, r_y, r_xy = 2 * y + 1 - x, 2 * (1 - y) + x, 3 - r
+    q = 2 * x + c
+    d = y * 4 + x * 2 + c
+
+    qkv_at = lambda rr, o, cs: qkv.at[at_rows(rr * 256 + cs * 128, 128, 128), at_rows(o * 384, 384, 128)]
+    wo_at = lambda rr, o, cs: wo.at[at_rows(o * 128, 128, 128), at_rows(rr * 256 + cs * 128, 128, 128)]
     s_pc = links.base("pc", 2)
-    links.put(qkv_in.at[:, at_rows((1 - c) * 384, 384, 128)], qkv_shard, s_pc, s_pc, to_c)
-    links.put(wo_in.at[at_rows((1 - c) * 128, 128, 128), :], wo_shard, s_pc + 1, s_pc + 1, to_c)
-    own_qkv = local(0, qkv_in.at[:, at_rows(c * 384, 384, 128)], qkv_shard)
-    own_wo = local(1, wo_in.at[at_rows(c * 128, 128, 128), :], wo_shard)
+    links.put(qkv_in.at[:, at_rows((1 - c) * 384, 384, 128)], qkv_at(r, z, c), s_pc, s_pc, to_c)
+    links.put(wo_in.at[at_rows((1 - c) * 128, 128, 128), :], wo_at(r, z, c), s_pc + 1, s_pc + 1, to_c)
+    own_qkv = local(0, qkv_in.at[:, at_rows(c * 384, 384, 128)], qkv_at(r, z, c))
+    own_wo = local(1, wo_in.at[at_rows(c * 128, 128, 128), :], wo_at(r, z, c))
     own_qkv.start()
     own_wo.start()
 
     s_norm, s_bias, s_mask = links.base("norm", 8), links.base("bias", 4), links.base("mask", 1)
-    d = y * 4 + x * 2 + c
     for dd in range(1, 8):
         to = place((y + dd // 4) % 2, (x + (dd // 2) % 2) % 2, (c + dd % 2) % 2, z)
         links.put(norm_in, norm.at[d], s_norm + dd, s_norm + dd, to)
@@ -425,125 +425,120 @@
             def _(j=j):
                 links.wait(target.at[pl.ds(j * Q, Q)], base + 2 + j, to_c)
 
-    move_tokens("tok", tok_in, lambda cc: tok, 5)
-
     up_shard = lambda sx, sc: up.at[at_rows(y * 512 + sx * 256 + sc * 128, 128, 128), at_rows(z * 256, 256, 128)]
     down_shard = lambda sx, sc: down.at[at_rows(z * 256, 256, 128), at_rows(y * 512 + sx * 256 + sc * 128, 128, 128)]
     s_up, s_down = links.base("up", 4), links.base("down", 4)
-    q = 2 * x + c
-    for dx, dc in ((1, 0), (1, 1), (0, 1)):
-        tx, tc = (x + dx) % 2, (c + dc) % 2
-        to, rel = place(y, tx, tc, z), 2 * dx + dc
-        links.put(w1_in.at[:, at_rows((2 * tx + tc) * 256, 256, 128)], up_shard(x, c), s_up + rel, s_up + rel, to)
-        links.put(w2_in.at[at_rows((2 * tx + tc) * 256, 256, 128), :], down_shard(x, c), s_down + rel, s_down + rel, to)
     own_up = local(6, w1_in.at[:, at_rows(q * 256, 256, 128)], up_shard(x, c))
     own_down = local(7, w2_in.at[at_rows(q * 256, 256, 128), :], down_shard(x, c))
     own_up.start()
     own_down.start()
 
-    class Line:
+    def part_up(dx, dc):
+        tx, tc, rel = (x + dx) % 2, (c + dc) % 2, 2 * dx + dc
+        to = place(y, tx, tc, z)
+        links.put(w1_in.at[:, at_rows((2 * tx + tc) * 256, 256, 128)], up_shard(x, c), s_up + rel, s_up + rel, to)
+
+    def part_down(dx, dc):
+        tx, tc, rel = (x + dx) % 2, (c + dc) % 2, 2 * dx + dc
+        to = place(y, tx, tc, z)
+        links.put(w2_in.at[at_rows((2 * tx + tc) * 256, 256, 128), :], down_shard(x, c), s_down + rel, s_down + rel, to)
+
+    def wait_parts(shard, base):
+        for dx, dc in ((0, 1), (1, 0), (1, 1)):
+            links.wait(shard((x + dx) % 2, (c + dc) % 2), base + 2 * dx + dc, to_c)
+
+    class Fan:
         def __init__(self, key, piece, arrived):
             self.piece, self.arrived = piece, arrived
-            self.many = many = len(piece(0))
-            self.got = [links.base((key, "got", n), 4) for n in range(many)]
-            self.up = [links.base((key, "up", n), 4) for n in range(many)]
-            self.down = [links.base((key, "down", n), 4) for n in range(many)]
-
-        def push(self, way_up, far):
-            def make(n):
-                o, there = self.origin(way_up, far)
-                ref = self.piece(o)[n]
-                sent = (self.up if way_up else self.down)[n] + o
-                onward = z < 3 if way_up else z > 0
-                when = onward if there is None else jnp.logical_and(there, onward)
-                return ref, ref, sent, self.got[n] + o, up_z if way_up else down_z, when
-
+            self.many = len(piece(0))
+            self.got = [links.base((key, "got", n), 4) for n in range(self.many)]
+            self.sent = [links.base((key, "sent", n), 3) for n in range(self.many)]
+
+        def push(self, slot, o, to):
             for n in range(self.many):
-                links.start(functools.partial(make, n))
-
-        def origin(self, way_up, far):
-            if far == 0:
-                return z, None
-            o = z - far if way_up else z + far
-            return jnp.clip(o, 0, 3), (o >= 0 if way_up else o < 4)
+                def make(n=n):
+                    ref = self.piece(o)[n]
+                    return ref, ref, self.sent[n] + slot, self.got[n] + o, to, None
+
+                links.start(make)
+
+        def take(self, o):
+            for n, ref in enumerate(self.piece(o)):
+                links.wait(ref, self.got[n] + o, to_z1)
 
         def begin(self):
-            self.push(True, 0)
-            self.push(False, 0)
-            self.arrived(functools.partial(self.origin, True, 0))
-
-        def step(self, far):
-            for way_up in (True, False):
-                o, there = self.origin(way_up, far)
-
-                @pl.when(there)
-                def _():
-                    for n, ref in enumerate(self.piece(o)):
-                        links.wait(ref, self.got[n] + o, up_z)
-
-                self.push(way_up, far)
-                self.arrived(functools.partial(self.origin, way_up, far))
-
-    s_first = [links.base(("first", n), 4) for n in range(2)]
-    s_own = [links.base(("own", n), 4) for n in range(2)]
-    s_fwd = [links.base(("fwd", n), 4) for n in range(2)]
-
-    def neighbours(o):
-        odd = o % 2
-        even = 1 - odd
-        y1, x1 = y + odd * (1 - 2 * y), x + even * (1 - 2 * x)
-        y2, x2 = y + even * (1 - 2 * y), x + odd * (1 - 2 * x)
-        return (y1, x1), (y2, x2)
-
-    def attn_arrived(origin):
-        o, there = origin()
-        (y1, x1), (y2, x2) = neighbours(o)
-        for n, ref in enumerate((qkv_at(r, o), wo_at(r, o))):
-            links.put(ref, ref, s_first[n] + o, s_first[n] + o, place(y1, x1, c, z), there)
-            links.put(ref, ref, s_own[n] + o, s_own[n] + o, place(y2, x2, c, z), there)
-
-    def attn_forward(o, there):
-        (y1, x1), (y2, x2) = neighbours(o)
-        r1 = 2 * y1 + x1
-        for n, ref in enumerate((qkv_at(r1, o), wo_at(r1, o))):
-            def arrive(n=n, ref=ref):
-                links.wait(ref, s_first[n] + o, to_x)
-
-            arrive() if there is None else pl.when(there)(arrive)
-
-            links.put(ref, ref, s_fwd[n] + o, s_fwd[n] + o, place(y2, x2, c, z), there)
+            self.push(0, z, to_z2)
+            self.push(1, z, to_z1)
+            self.arrived(z)
+
+        def far(self):
+            self.take(z2)
+            self.push(2, z2, to_z1)
+            self.arrived(z2)
+
+        def pair(self):
+            self.take(z1)
+            self.arrived(z1)
+
+        def diagonal(self):
+            self.take(z3)
+            self.arrived(z3)
+
+    attn_at = (qkv_at, wo_at)
+    s_first = [links.base(("first", n), 8) for n in range(2)]
+    s_own = [links.base(("own", n), 8) for n in range(2)]
+    s_fwd = [links.base(("fwd", n), 8) for n in range(2)]
+    to_first, to_second = (to_x, to_y), (to_y, to_x)
+    r_first, r_second = (r_x, r_y), (r_y, r_x)
+
+    def attn_arrived(o):
+        for n, at in enumerate(attn_at):
+            for cs in range(2):
+                ref, sem = at(r, o, cs), o * 2 + cs
+                links.put(ref, ref, s_first[n] + sem, s_first[n] + sem, to_first[cs])
+        for n, at in enumerate(attn_at):
+            for cs in range(2):
+                ref, sem = at(r, o, cs), o * 2 + cs
+                links.put(ref, ref, s_own[n] + sem, s_own[n] + sem, to_second[cs])
+
+    def attn_forward(o):
+        for n, at in enumerate(attn_at):
+            for cs in range(2):
+                ref, sem = at(r_first[cs], o, cs), o * 2 + cs
+                links.wait(ref, s_first[n] + sem, to_x)
+                links.put(ref, ref, s_fwd[n] + sem, s_fwd[n] + sem, to_second[cs])
 
     def attn_finish():
         for o in range(4):
-            (y1, x1), (y2, x2) = neighbours(o)
-            for n, at in enumerate((qkv_at, wo_at)):
-                links.wait(at(2 * y2 + x2, o), s_own[n] + o, to_x)
-                links.wait(at(2 * (1 - y) + 1 - x, o), s_fwd[n] + o, to_x)
-
-    attn_line = Line("attn", lambda o: (qkv_at(r, o), wo_at(r, o)), attn_arrived)
+            for n, at in enumerate(attn_at):
+                for cs in range(2):
+                    sem = o * 2 + cs
+                    links.wait(at(r_second[cs], o, cs), s_own[n] + sem, to_x)
+                    links.wait(at(r_xy, o, cs), s_fwd[n] + sem, to_x)
+
+    attn_fan = Fan("attn", lambda o: [at(r, o, cs) for at in attn_at for cs in range(2)], attn_arrived)
     up_at = lambda yy, o: up.at[at_rows(yy * 512, 512, 512), at_rows(o * 256, 256, 256)]
     down_at = lambda yy, o: down.at[at_rows(o * 256, 256, 256), at_rows(yy * 512, 512, 512)]
     s_upy, s_downy = links.base("upy", 4), links.base("downy", 4)
 
     def across(at, base):
-        def arrived(origin):
-            def make():
-                o, there = origin()
-                return at(y, o), at(y, o), base + o, base + o, to_y, there
-
-            links.start(make)
-
-        return arrived
-
-    up_line = Line("upl", lambda o: (up_at(y, o),), across(up_at, s_upy))
-    down_line = Line("downl", lambda o: (down_at(y, o),), across(down_at, s_downy))
+        return lambda o: links.start(lambda: (at(y, o), at(y, o), base + o, base + o, to_y, None))
+
+    up_fan = Fan("upf", lambda o: (up_at(y, o),), across(up_at, s_upy))
+    down_fan = Fan("downf", lambda o: (down_at(y, o),), across(down_at, s_downy))
 
     lse[...] = jnp.zeros_like(lse)
     own_qkv.wait()
     own_wo.wait()
-    links.wait(qkv_other, s_pc, to_c)
-    links.wait(wo_other, s_pc + 1, to_c)
-    attn_line.begin()
+    links.wait(qkv_at(r, z, 1 - c), s_pc, to_c)
+    links.wait(wo_at(r, z, 1 - c), s_pc + 1, to_c)
+    attn_fan.begin()
+    attn_fan.far()
+    attn_forward(z)
+    move_tokens("tok", tok_in, lambda cc: tok, 5)
+    for dx, dc in ((1, 0), (1, 1), (0, 1)):
+        part_up(dx, dc)
+    attn_fan.pair()
     for one in own_small:
         one.wait()
     for dd in range(1, 8):
@@ -560,11 +555,16 @@
         qkv_row[:, zz * 384 + 256 : zz * 384 + 384] = bias[zz, 1:2]
         up_row[:, zz * 256 : zz * 256 + 128] = bias[zz, 2:3]
         up_row[:, zz * 256 + 128 : zz * 256 + 256] = bias[zz, 3:4]
-
+    attn_fan.diagonal()
+    attn_forward(z2)
+    attn_forward(z1)
+    for dx, dc in ((1, 0), (1, 1), (0, 1)):
+        part_down(dx, dc)
     own_up.wait()
     own_down.wait()
-    attn_line.step(1)
-    attn_forward(z, None)
+    wait_parts(up_shard, s_up)
+    up_fan.begin()
+    attn_forward(z3)
 
     wait_tokens("tok", tok_in, lambda cc: tok, 5)
 
@@ -577,28 +577,13 @@
     s_n1 = links.base("n1", 1)
     half_at = lambda ref, cc: ref.at[at_rows(cc * HALF, HALF, 64), :]
     links.put(half_at(n1, c), half_at(n1, c), s_n1, s_n1, to_c)
-
-    def forward_far(far):
-        attn_forward(jnp.clip(z - far, 0, 3), z >= far)
-        attn_forward(jnp.clip(z + far, 0, 3), z + far < 4)
-
-    attn_line.step(2)
-    forward_far(1)
-    attn_line.step(3)
-    for dx, dc in ((1, 0), (1, 1), (0, 1)):
-        rel, sx, sc = 2 * dx + dc, (x + dx) % 2, (c + dc) % 2
-        links.wait(up_shard(sx, sc), s_up + rel, to_c)
-    up_line.begin()
-    forward_far(2)
+    up_fan.far()
     move_tokens("cot", cot_in, lambda cc: block_at(cot, 2 * x + cc), 8)
-    for dx, dc in ((1, 0), (1, 1), (0, 1)):
-        rel, sx, sc = 2 * dx + dc, (x + dx) % 2, (c + dc) % 2
-        links.wait(down_shard(sx, sc), s_down + rel, to_c)
-    up_line.step(1)
-    forward_far(3)
-    down_line.begin()
+    wait_parts(down_shard, s_down)
     links.wait(half_at(n1, 1 - c), s_n1, to_c)
     attn_finish()
+    up_fan.pair()
+    down_fan.begin()
 
     @pl.loop(0, 6)
     def _(j):
@@ -608,7 +593,23 @@
     lane = lax.broadcasted_iota(jnp.int32, (1, 128), 1)
     first_head = lane < 64
     zero = jnp.zeros((), BF)
-    up_line.step(2)
+
+    def spread_start(key, ref):
+        base = links.base(("spread", key), 3)
+        links.start(lambda: (block_at(ref, q), block_at(ref, q), base, base, to_x, None))
+        links.start(lambda: (block_at(ref, q), block_at(ref, q), base + 1, base + 1, to_c, None))
+
+    def spread_forward(key, ref):
+        base = links.base(("spread", key), 3)
+        far = lambda: block_at(ref, 2 * (1 - x) + c)
+        links.wait(far(), base, to_x)
+        links.start(lambda: (far(), far(), base + 2, base + 2, to_c, None))
+
+    def spread_wait_near(key, ref):
+        links.wait(block_at(ref, 2 * x + 1 - c), links.base(("spread", key), 3) + 1, to_c)
+
+    def spread_wait_far(key, ref):
+        links.wait(block_at(ref, 2 * (1 - x) + 1 - c), links.base(("spread", key), 3) + 2, to_c)
 
     @pl.loop(0, 4)
     def _(zz):
@@ -633,17 +634,16 @@
 
         @pl.when(zz == 0)
         def _():
-            down_line.step(1)
-
-        @pl.when(zz == 1)
-        def _():
-            up_line.step(3)
+            up_fan.diagonal()
 
         @pl.when(zz == 2)
         def _():
-            down_line.step(2)
-
-    down_line.step(3)
+            down_fan.far()
+
+        @pl.when(zz == 3)
+        def _():
+            wait_tokens("cot", cot_in, lambda cc: block_at(cot, 2 * x + cc), 8)
+            spread_start("cot", cot)
 
     s_part = links.base("part", 1)
 
@@ -666,26 +666,10 @@
         unit, _ = unit_rows(v)
         n2[block_rows(q, i * 32, 32), :] = (unit * norm_row[1:2] + norm_row[3:4]).astype(BF)
 
-    def spread_start(key, ref):
-        base = links.base(("spread", key), 3)
-        links.put(block_at(ref, q), block_at(ref, q), base, base, to_x)
-        links.put(block_at(ref, q), block_at(ref, q), base + 1, base + 1, to_c)
-
-    def spread_forward(key, ref):
-        base = links.base(("spread", key), 3)
-        far = block_at(ref, 2 * (1 - x) + c)
-        links.wait(far, base, to_x)
-        links.put(far, far, base + 2, base + 2, to_c)
-
-    def spread_wait_near(key, ref):
-        links.wait(block_at(ref, 2 * x + 1 - c), links.base(("spread", key), 3) + 1, to_c)
-
-    def spread_wait_far(key, ref):
-        links.wait(block_at(ref, 2 * (1 - x) + 1 - c), links.base(("spread", key), 3) + 2, to_c)
-
     spread_start("n2", n2)
-    wait_tokens("cot", cot_in, lambda cc: block_at(cot, 2 * x + cc), 8)
-    spread_start("cot", cot)
+    down_fan.pair()
+    spread_forward("cot", cot)
+    spread_wait_near("cot", cot)
     for o in range(4):
         links.wait(up_at(1 - y, o), s_upy + o, to_y)
 
@@ -703,15 +687,12 @@
     expand(q)
     spread_wait_near("n2", n2)
     expand(2 * x + 1 - c)
+    down_fan.diagonal()
     spread_forward("n2", n2)
     expand(2 * (1 - x) + c)
     spread_wait_far("n2", n2)
     expand(2 * (1 - x) + 1 - c)
-    spread_wait_near("cot", cot)
-    spread_forward("cot", cot)
     spread_wait_far("cot", cot)
-    for o in range(4):
-        links.wait(down_at(1 - y, o), s_downy + o, to_y)
 
     near_other, far_own, far_other = 2 * x + 1 - c, 2 * (1 - x) + c, 2 * (1 - x) + 1 - c
     sums[...] = jnp.zeros_like(sums)
@@ -749,6 +730,88 @@
             for source in sources[1:]:
                 total = total + source[rows, :].astype(F32)
             target[rows, :] = total.astype(target.dtype)
+
+    z_order = (z3, z1, z2, z)
+    s_rdown, s_rup = links.base("rdown", 4), links.base("rup", 4)
+    d_down_at = lambda yy, o: d_down.at[at_rows(o * 256, 256, 256), at_rows(yy * 512, 512, 512)]
+    d_up_at = lambda yy, o: d_up.at[at_rows(yy * 512, 512, 512), at_rows(o * 256, 256, 256)]
+    r_down_at = lambda o: r_down.at[at_rows(o * 256, 256, 256), :]
+    r_up_at = lambda o: r_up.at[:, at_rows(o * 256, 256, 256)]
+
+    def accumulate(target, *sources):
+        count = target.shape[0] // 64
+
+        @pl.loop(0, count)
+        def _(i):
+            rows = at_rows(i * 64, 64, 64)
+            total = target[rows, :].astype(F32)
+            for source in sources:
+                total = total + source[rows, :].astype(F32)
+            target[rows, :] = total.astype(target.dtype)
+
+    class Fold:
+        def __init__(self, key, piece, over_z, final):
+            self.piece, self.over_z, self.final = piece, over_z, final
+            self.sz = links.base((key, "z"), 3)
+
+        def push(self, o, slot, to):
+            links.start(lambda: (self.piece(o), self.over_z.at[slot], self.sz + slot, self.sz + slot, to, None))
+
+        def pair_far(self):
+            self.collect(z3)
+            self.push(z3, 0, to_z1)
+
+        def pair_near(self):
+            self.collect(z1)
+            self.push(z1, 1, to_z1)
+
+        def far(self):
+            self.collect(z2)
+            links.wait(self.over_z.at[0], self.sz, to_z1)
+            accumulate(self.piece(z2), self.over_z.at[0])
+            self.push(z2, 2, to_z2)
+
+        def last(self):
+            self.collect(z)
+            links.wait(self.over_z.at[1], self.sz + 1, to_z1)
+            links.wait(self.over_z.at[2], self.sz + 2, to_z2)
+            own, others = self.piece(z), [self.over_z.at[1], self.over_z.at[2]]
+            count = own.shape[0] // 64
+
+            @pl.loop(0, count)
+            def _(i):
+                rows = at_rows(i * 64, 64, 64)
+                total = own[rows, :].astype(F32)
+                for other in others:
+                    total = total + other[rows, :].astype(F32)
+                self.final[rows, :] = total.astype(BF)
+
+    class Half(Fold):
+        def __init__(self, key, at, got_at, s_got, over_z, final):
+            super().__init__(key, lambda o: at(y, o), over_z, final)
+            self.got_at, self.s_got = got_at, s_got
+
+        def collect(self, o):
+            links.wait(self.got_at(o), self.s_got + o, to_y)
+            accumulate(self.piece(o), self.got_at(o))
+
+    half_down = Half("half_down", d_down_at, r_down_at, s_rdown, z_down, f_down)
+    half_up = Half("half_up", d_up_at, r_up_at, s_rup, z_up, f_up)
+
+    def give_down(o):
+        rows = at_rows(o * 256, 256, 256)
+        d_down[rows, :] = mm(act[:, rows], cot[...], TN).astype(BF)
+        links.start(lambda: (d_down_at(1 - y, o), r_down_at(o), s_rdown + o, s_rdown + o, to_y, None))
+
+    def give_up(o):
+        columns = at_rows(o * 256, 256, 256)
+        d_up[:, columns] = mm(n2[...], slope[:, columns], TN).astype(BF)
+        links.start(lambda: (d_up_at(1 - y, o), r_up_at(o), s_rup + o, s_rup + o, to_y, None))
+
+    for o in z_order:
+        give_down(o)
+    for o in range(4):
+        links.wait(down_at(1 - y, o), s_downy + o, to_y)
 
     s_gfar, s_gmid, s_gnear = links.base("gfar", 1), links.base("gmid", 1), links.base("gnear", 1)
     s_bfar, s_bmid, s_bnear = links.base("bfar", 1), links.base("bmid", 1), links.base("bnear", 1)
@@ -767,29 +830,11 @@
     links.put(s_near, g_near, s_gnear, s_gnear, to_c)
     through_slope(q)
     back_part(q, part)
-
-    s_rdown, s_rup = links.base("rdown", 4), links.base("rup", 4)
-    d_down_at = lambda yy, o: d_down.at[at_rows(o * 256, 256, 256), at_rows(yy * 512, 512, 512)]
-    d_up_at = lambda yy, o: d_up.at[at_rows(yy * 512, 512, 512), at_rows(o * 256, 256, 256)]
-    r_down_at = lambda o: r_down.at[at_rows(o * 256, 256, 256), :]
-    r_up_at = lambda o: r_up.at[:, at_rows(o * 256, 256, 256)]
-
-    def make_rdown(k):
-        o = (z + 1 + k) % 4
-        return d_down_at(1 - y, o), r_down_at(o), s_rdown + o, s_rdown + o, to_y, None
-
-    def make_rup(k):
-        o = (z + 1 + k) % 4
-        return d_up_at(1 - y, o), r_up_at(o), s_rup + o, s_rup + o, to_y, None
-
-    for k in range(4):
-        rows = at_rows(((z + 1 + k) % 4) * 256, 256, 256)
-        d_down[rows, :] = mm(act[:, rows], cot[...], TN).astype(BF)
-        links.start(functools.partial(make_rdown, k))
-    for k in range(4):
-        columns = at_rows(((z + 1 + k) % 4) * 256, 256, 256)
-        d_up[:, columns] = mm(n2[...], slope[:, columns], TN).astype(BF)
-        links.start(functools.partial(make_rup, k))
+    half_down.pair_far()
+    half_down.pair_near()
+    for o in z_order:
+        give_up(o)
+    half_down.far()
 
     links.wait(g_near, s_gnear, to_c)
     links.wait(g_mid, s_gmid, to_x)
@@ -843,102 +888,49 @@
         columns = at_rows(j * 256, 256, 256)
         d_wo[columns, :] = mm(mix[:, columns], ga[...], TN).astype(BF)
 
-    d_qkv_at = lambda rr, o: d_qkv.at[at_rows(rr * 256, 256, 256), at_rows(o * 384, 384, 128)]
-    d_wo_at = lambda rr, o: d_wo.at[at_rows(o * 128, 128, 128), at_rows(rr * 256, 256, 128)]
-
-    def accumulate(target, *sources):
-        count = target.shape[0] // 64
-
-        @pl.loop(0, count)
-        def _(i):
-            rows = at_rows(i * 64, 64, 64)
-            total = target[rows, :].astype(F32)
-            for source in sources:
-                total = total + source[rows, :].astype(F32)
-            target[rows, :] = total.astype(target.dtype)
-
-    class Reduce:
-        def __init__(self, key, at, first, second, over_z, final):
-            self.at, self.first, self.second, self.over_z, self.final = at, first, second, over_z, final
-            self.s1 = [links.base((key, "first", i), 4) for i in range(2)]
-            self.s2, self.sz = links.base((key, "second"), 4), links.base((key, "z"), 8)
-
-        def begin(self, o):
-            def make(i):
-                (y1, x1), (y2, x2) = neighbours(o)
-                rr = 2 * y1 + x1 if i == 0 else 3 - r
-                return self.at(rr, o), self.first.at[i, o], self.s1[i] + o, self.s1[i] + o, place(y1, x1, c, z), None
-
-            for i in (1, 0):
-                links.start(functools.partial(make, i))
-
-        def middle(self, o):
-            (y1, x1), (y2, x2) = neighbours(o)
-            links.wait(self.first.at[1, o], self.s1[1] + o, to_x)
-            accumulate(self.at(2 * y2 + x2, o), self.first.at[1, o])
-
-            def make():
-                (y1, x1), (y2, x2) = neighbours(o)
-                return self.at(2 * y2 + x2, o), self.second.at[o], self.s2 + o, self.s2 + o, place(y2, x2, c, z), None
-
-            links.start(make)
-
-        def gather(self, k):
-            o = (z + 1 + k) % 4
-            links.wait(self.first.at[0, o], self.s1[0] + o, to_x)
-            links.wait(self.second.at[o], self.s2 + o, to_x)
-            accumulate(self.at(r, o), self.first.at[0, o], self.second.at[o])
-            if k < 3:
-                push_z(self, k, lambda o: self.at(r, o))
-
-        def last(self):
-            finish_z(self, self.at(r, z))
-
-    def push_z(owner, k, at):
-        def make():
-            o = (z + 1 + k) % 4
-            return at(o), owner.over_z.at[z], owner.sz + k, owner.sz + 4 + z, place(y, x, c, o), None
-
-        links.start(make)
-
-    def finish_z(owner, own):
-        for k in range(3):
-            source = (z + 1 + k) % 4
-            links.wait(owner.over_z.at[source], owner.sz + 4 + source, up_z_other)
-        others = [owner.over_z.at[(z + 1 + k) % 4] for k in range(3)]
-        count = own.shape[0] // 64
-
-        @pl.loop(0, count)
-        def _(i):
-            rows = at_rows(i * 64, 64, 64)
-            total = own[rows, :].astype(F32)
-            for other in others:
-                total = total + other[rows, :].astype(F32)
-            owner.final[rows, :] = total.astype(BF)
-
-    up_z_other = to_c
-    red_wo = Reduce("red_wo", d_wo_at, first_wo, second_wo, z_wo, f_wo)
-    red_qkv = Reduce("red_qkv", d_qkv_at, first_qkv, second_qkv, z_qkv, f_qkv)
-    for o in range(4):
-        red_wo.begin(o)
-
-    class Half:
-        def __init__(self, key, at, got_at, s_got, over_z, final):
-            self.at, self.got_at, self.s_got, self.over_z, self.final = at, got_at, s_got, over_z, final
-            self.sz = links.base((key, "z"), 8)
-
-        def gather(self, k):
-            o = (z + 1 + k) % 4
-            links.wait(self.got_at(o), self.s_got + o, to_y)
-            accumulate(self.at(y, o), self.got_at(o))
-            if k < 3:
-                push_z(self, k, lambda o: self.at(y, o))
-
-        def last(self):
-            finish_z(self, self.at(y, z))
-
-    half_down = Half("half_down", d_down_at, r_down_at, s_rdown, z_down, f_down)
-    half_up = Half("half_up", d_up_at, r_up_at, s_rup, z_up, f_up)
+    d_qkv_at = lambda rr, o, cs: d_qkv.at[at_rows(rr * 256 + cs * 128, 128, 128), at_rows(o * 384, 384, 128)]
+    d_wo_at = lambda rr, o, cs: d_wo.at[at_rows(o * 128, 128, 128), at_rows(rr * 256 + cs * 128, 128, 128)]
+    d_qkv_all = lambda o: d_qkv.at[at_rows(r * 256, 256, 256), at_rows(o * 384, 384, 128)]
+    d_wo_all = lambda o: d_wo.at[at_rows(o * 128, 128, 128), at_rows(r * 256, 256, 128)]
+
+    class Reduce(Fold):
+        def __init__(self, key, at, whole, first, second, over_z, final):
+            super().__init__(key, whole, over_z, final)
+            self.at, self.first, self.second = at, first, second
+            self.s1 = [links.base((key, "first", i), 8) for i in range(2)]
+            self.s2 = links.base((key, "second"), 8)
+
+        def begin(self, o, cs):
+            sem = 2 * o + cs
+            for i, rr in ((1, r_xy), (0, r_first[cs])):
+                links.start(
+                    lambda i=i, rr=rr: (
+                        self.at(rr, o, cs), self.first.at[i, o, cs], self.s1[i] + sem, self.s1[i] + sem, to_first[cs], None,
+                    )
+                )
+
+        def middle(self, o, cs):
+            sem = 2 * o + cs
+            links.wait(self.first.at[1, o, cs], self.s1[1] + sem, to_x)
+            accumulate(self.at(r_second[cs], o, cs), self.first.at[1, o, cs])
+            links.start(
+                lambda: (
+                    self.at(r_second[cs], o, cs), self.second.at[o, cs], self.s2 + sem, self.s2 + sem, to_second[cs], None,
+                )
+            )
+
+        def collect(self, o):
+            for cs in range(2):
+                sem = 2 * o + cs
+                links.wait(self.first.at[0, o, cs], self.s1[0] + sem, to_x)
+                links.wait(self.second.at[o, cs], self.s2 + sem, to_x)
+                accumulate(self.at(r, o, cs), self.first.at[0, o, cs], self.second.at[o, cs])
+
+    red_wo = Reduce("red_wo", d_wo_at, d_wo_all, first_wo, second_wo, z_wo, f_wo)
+    red_qkv = Reduce("red_qkv", d_qkv_at, d_qkv_all, first_qkv, second_qkv, z_qkv, f_qkv)
+    for cs in range(2):
+        for o in z_order:
+            red_wo.begin(o, cs)
 
     down_part(far_own, part)
     links.wait(b_far, s_bfar, to_c)
@@ -947,6 +939,26 @@
     down_part(near_other, s_near)
     links.put(s_near, b_near, s_bnear, s_bnear, to_c)
     down_part(q, hid, hid)
+
+    s_oup, s_odown = links.base("oup", 4), links.base("odown", 4)
+
+    def scatter_down():
+        for dx, dc in ((1, 0), (1, 1), (0, 1)):
+            def make(dx=dx, dc=dc):
+                rel, tx, tc = 2 * dx + dc, (x + dx) % 2, (c + dc) % 2
+                columns = at_rows((2 * tx + tc) * 128, 128, 128)
+                return f_down.at[:, columns], o_down.at[q], s_odown + rel, s_odown + rel, place(y, tx, tc, z), None
+
+            links.start(make)
+
+    def scatter_up():
+        for dx, dc in ((1, 0), (1, 1), (0, 1)):
+            def make(dx=dx, dc=dc):
+                rel, tx, tc = 2 * dx + dc, (x + dx) % 2, (c + dc) % 2
+                rows = at_rows((2 * tx + tc) * 128, 128, 128)
+                return f_up.at[rows, :], o_up.at[q], s_oup + rel, s_oup + rel, place(y, tx, tc, z), None
+
+            links.start(make)
 
     @pl.loop(0, 4)
     def _(zz):
@@ -986,18 +998,17 @@
 
         @pl.when(zz == 0)
         def _():
-            for o in range(4):
-                red_wo.middle(o)
+            half_down.last()
+            scatter_down()
 
         @pl.when(zz == 1)
         def _():
-            for k in range(4):
-                half_down.gather(k)
+            half_up.pair_far()
+            half_up.pair_near()
 
         @pl.when(zz == 2)
         def _():
-            for k in range(4):
-                half_up.gather(k)
+            half_up.far()
 
     links.wait(b_near, s_bnear, to_c)
     links.wait(b_mid, s_bmid, to_x)
@@ -1044,13 +1055,13 @@
     def weigh(rr):
         d_qkv[at_rows(rr * 256, 256, 256), :] = mm(n1[:, at_rows(rr * 256, 256, 256)], gproj[...], TN).astype(BF)
 
-    weigh(3 - r)
-    weigh(2 * y + 1 - x)
-    red_qkv.begin(0)
-    red_qkv.begin(2)
-    weigh(2 * (1 - y) + x)
-    red_qkv.begin(1)
-    red_qkv.begin(3)
+    weigh(r_xy)
+    weigh(r_x)
+    for o in z_order:
+        red_qkv.begin(o, 0)
+    weigh(r_y)
+    for o in z_order:
+        red_qkv.begin(o, 1)
 
     def front_part(cc, target):
         @pl.loop(0, 4)
@@ -1061,6 +1072,9 @@
     s_gn1 = links.base("gn1", 1)
     front_part(1 - c, s_far)
     links.put(s_far, g_n1, s_gn1, s_gn1, to_c)
+    for o in z_order:
+        for cs in range(2):
+            red_wo.middle(o, cs)
     weigh(r)
     front_part(c, part)
     links.wait(g_n1, s_gn1, to_c)
@@ -1111,10 +1125,17 @@
 
         links.start(make)
 
-    for o in range(4):
-        red_qkv.middle(o)
-    for k in range(4):
-        red_wo.gather(k)
+    half_up.last()
+    scatter_up()
+    red_wo.pair_far()
+    red_wo.pair_near()
+    for o in z_order:
+        for cs in range(2):
+            red_qkv.middle(o, cs)
+    red_wo.far()
+    red_qkv.pair_far()
+    red_qkv.pair_near()
+    red_qkv.far()
 
     for dz in range(1, 4):
         links.wait(bias_got.at[dz], s_bz + dz, to_c)
@@ -1137,27 +1158,6 @@
 
         links.start(make)
 
-    half_down.last()
-    half_up.last()
-    s_oup, s_odown = links.base("oup", 4), links.base("odown", 4)
-    for dx, dc in ((1, 0), (1, 1), (0, 1)):
-        rel = 2 * dx + dc
-
-        def make_up(dx=dx, dc=dc, rel=rel):
-            tx, tc = (x + dx) % 2, (c + dc) % 2
-            rows = at_rows((2 * tx + tc) * 128, 128, 128)
-            return f_up.at[rows, :], o_up.at[q], s_oup + rel, s_oup + rel, place(y, tx, tc, z), None
-
-        def make_down(dx=dx, dc=dc, rel=rel):
-            tx, tc = (x + dx) % 2, (c + dc) % 2
-            columns = at_rows((2 * tx + tc) * 128, 128, 128)
-            return f_down.at[:, columns], o_down.at[q], s_odown + rel, s_odown + rel, place(y, tx, tc, z), None
-
-        links.start(make_up)
-        links.start(make_down)
-
-    for k in range(4):
-        red_qkv.gather(k)
     red_wo.last()
 
     w1_out[:, at_rows(q * 256, 256, 256)] = f_up[at_rows(q * 128, 128, 128), :].astype(F32)
@@ -1233,10 +1233,10 @@
         wide(8, 1024), wide(1, 1536), wide(1, 1024), wide(HALF, 1024), wide(HALF, 1024),
         low(FULL, 1024), low(FULL, 512), low(FULL, 1536),
         low(1024, 1024), low(1024, 1024), low(1024, 1536), low(512, 1024),
-        low(512, 1024), low(1024, 512), low(4, 512, 256), low(4, 256, 512),
+        low(512, 1024), low(1024, 512), low(3, 512, 256), low(3, 256, 512),
         low(512, 256), low(256, 512), low(4, 128, 256), low(4, 256, 128),
-        low(2, 4, 256, 384), low(2, 4, 128, 256), low(4, 256, 384), low(4, 128, 256),
-        low(4, 256, 384), low(4, 128, 256), low(256, 384), low(128, 256), low(128, 384), low(128, 128),
+        low(2, 4, 2, 128, 384), low(2, 4, 2, 128, 128), low(4, 2, 128, 384), low(4, 2, 128, 128),
+        low(3, 256, 384), low(3, 128, 256), low(256, 384), low(128, 256), low(128, 384), low(128, 128),
         *[low(HALF, 1024)] * 10,
         wide(48, 1024), wide(8, 1024), wide(8, 8, 128), wide(4, 8, 128),
         wide(8, 1024), wide(8, 512), wide(8, 512), wide(4, 8, 128), wide(4, 8, 128), wide(8, 8, 128),

time: 311 us -> 244 us (0.78)
  Pallas kernels: 287 us -> 222 us
    pallas_call x1, Pallas kernels: 287 us -> 222 us  [layer_call(): pl.pallas_call(layer_kernel, out_shape=outs, in_specs=[hbm] * 9, out_spec...]
where the time goes in v1:
time: 244 us
  Pallas kernels  222 us (91%)
  local copies, waits for them, and re-layouts  17.8 us (7%)
  other arithmetic  2.73 us (1%)
    pallas_call x1, Pallas kernels, layer_call(): pl.pallas_call(layer_kernel, out_shape=outs, in_specs=[hbm] * 9, out_spec...  222 us
    unnamed x29, local copies, waits for them, and re-layouts  9.11 us

profile of v1, /device:TPU:1, one launch (start us, length us, event | category | flops | bytes accessed | tf_op | source)
XLA Modules:
  0.0 243.5 jit_solution(7393422965218708425)
XLA Ops:
  0.6 0.0 copy-start
  0.7 0.8 dynamic-slice_bitcast_fusion
  1.5 0.7 constant_dynamic-slice_fusion
  2.2 0.6 fusion.7.bias_in
  2.8 1.3 fusion.5.norm_in
  4.0 0.7 compare_select_fusion
  4.7 0.1 select_n.29
  4.8 0.7 reshape.47.mask_in
  5.5 1.1 copy.35
  6.6 0.8 copy.37.qkv_in
  7.5 0.0 copy-done
  7.5 0.0 copy-start.1
  7.5 0.1 copy.46
  7.6 0.9 pad.23.tok_in
  8.5 0.0 copy-done.1
  8.5 0.1 copy.45
  8.7 0.9 pad.24.cot_in
  9.6 222.2 %layer.1 = (bf16[2,160,1024]{2,1,0:T(8,128)(2,1)}, bf16[2,160,1024]{2,1,0:T(8,128)(2,1)}, f32[8,128]{1,0:T(8,128)}, f32[2,256]{1,0:T(2,128)}, f32[8,128]{1,0:T(8...) custom-call(bf16[2,160,1024]{2,1,0:T(8,128)(2,1)} %pad.23.tok_in, ...), custom_call_target="tpu_custom_call" | custom-call | tf_op jit(solution)/shard_map/layer/pallas_call | solution.py:1245
  231.8 0.0 copy-start.2
  231.8 0.0 copy-start.3
  231.8 1.3 slice.14
  233.2 1.3 slice.15
  234.4 1.1 copy.38
  235.6 0.9 copy.42
  236.5 0.0 copy-done.2
  236.5 0.0 copy-done.3
  236.5 0.2 convert_bitcast_fusion
  236.7 0.0 copy-start.8
  236.7 0.0 copy-start.6
  236.7 1.9 copy.41
  238.7 0.0 copy-start.5
  238.7 0.0 copy-start.7
  238.7 0.0 copy-start.4
  238.7 1.4 copy.40
  240.1 0.0 copy-done.8
  240.1 0.6 copy.52
  240.7 0.0 copy-done.6
  240.7 0.7 copy.53
  241.3 0.0 copy-done.5
  241.3 0.8 copy.54
  242.1 0.0 copy-done.7
  242.1 0.6 copy.55
  242.7 0.0 copy-done.4
  242.7 0.8 copy.56
  (3 shorter events, 0.1 us)
Async XLA Ops:
  0.6 6.8 %copy-start = (bf16[146,2,1024]{2,1,0:T(2,128)(2,1)S(1)}, bf16[146,2,1024]{2,1,0:T(2,128)(2,1)}, u32[]{:S(2)}) copy-start(bf16[146,2,1024]{2,1,0:T(2,128)(2,1)} %param.11) | copy-start | bytes 1794052
  7.5 1.1 copy-start.1
  231.8 4.7 %copy-start.2 = (bf16[2,160,1024]{2,1,0:T(8,128)(2,1)S(1)}, bf16[2,160,1024]{2,1,0:T(8,128)(2,1)}, u32[]{:S(2)}) copy-start(bf16[2,160,1024]{2,1,0:T(8,128)(2,1)} %get-tuple-element.19) | copy-start | bytes 1966084
  231.8 4.7 %copy-start.3 = (bf16[2,160,1024]{2,1,0:T(8,128)(2,1)S(1)}, bf16[2,160,1024]{2,1,0:T(8,128)(2,1)}, u32[]{:S(2)}) copy-start(bf16[2,160,1024]{2,1,0:T(8,128)(2,1)} %get-tuple-element.20) | copy-start | bytes 1966084
  236.7 3.4 %copy-start.8 = (f32[2,256]{1,0:T(2,128)S(1)}, f32[2,256]{1,0:T(2,128)}, u32[]{:S(2)}) copy-start(f32[2,256]{1,0:T(2,128)} %get-tuple-element.75) | copy-start | bytes 6148
  236.7 4.0 %copy-start.6 = (f32[256,128]{1,0:T(8,128)S(1)}, f32[256,128]{1,0:T(8,128)}, u32[]{:S(2)}) copy-start(f32[256,128]{1,0:T(8,128)} %get-tuple-element.76) | copy-start | bytes 393220
  238.7 2.7 %copy-start.5 = (f32[128,1024]{1,0:T(8,128)S(1)}, f32[128,1024]{1,0:T(8,128)}, u32[]{:S(2)}) copy-start(f32[128,1024]{1,0:T(8,128)} %get-tuple-element.77) | copy-start | bytes 1572868
  238.7 3.5 %copy-start.7 = (f32[8,128]{1,0:T(8,128)S(1)}, f32[8,128]{1,0:T(8,128)}, u32[]{:S(2)}) copy-start(f32[8,128]{1,0:T(8,128)} %get-tuple-element.26) | copy-start | bytes 12292
  238.7 4.1 %copy-start.4 = (f32[1024,128]{1,0:T(8,128)S(1)}, f32[1024,128]{1,0:T(8,128)}, u32[]{:S(2)}) copy-start(f32[1024,128]{1,0:T(8,128)} %get-tuple-element.79) | copy-start | bytes 1572868

commit v2 on v1

--- a/solution.py
+++ b/solution.py
@@ -243,6 +243,7 @@
 
 
 Q = 160
+SENT = 152
 HALF = 2 * Q
 FULL = 4 * Q
 BF, F32 = jnp.bfloat16, jnp.float32
@@ -266,29 +267,42 @@
 TN = ((0,), (0,))
 
 
+class Index:
+    def __init__(self, links, key, count, offset=0):
+        self.links, self.key, self.count, self.offset = links, key, count, offset
+
+    def __add__(self, more):
+        return Index(self.links, self.key, self.count, self.offset + more)
+
+    def place(self, table):
+        if self.key not in table:
+            table[self.key] = table["next"]
+            table["next"] += self.count
+        return table[self.key] + self.offset
+
+
 class Links:
     def __init__(self, send_sem, recv_sem):
         self.send_sem, self.recv_sem = send_sem, recv_sem
-        self.sends, self.used, self.keys, self.dropped = [], 0, {}, set()
+        self.sends, self.counts, self.dropped = [], {}, set()
+        self.sent_at, self.got_at = {"next": 0}, {"next": 0}
 
     def base(self, key, count):
-        if key not in self.keys:
-            self.keys[key] = self.used
-            self.used += count
-        return self.keys[key]
+        count = self.counts.setdefault(key, count)
+        return Index(self, key, count)
 
     def copy(self, src, dst, sent, got, to):
         return pltpu.make_async_remote_copy(
             src_ref=src,
             dst_ref=dst,
-            send_sem=self.send_sem.at[sent],
-            recv_sem=self.recv_sem.at[got],
+            send_sem=self.send_sem.at[0 if sent is None else sent.place(self.sent_at)],
+            recv_sem=self.recv_sem.at[got.place(self.got_at)],
             device_id=to,
             device_id_type=MESH,
         )
 
     def drop(self, *sent):
-        self.dropped = self.dropped | set(sent)
+        self.dropped = self.dropped | {(one.key, one.offset) for one in sent}
 
     def each(self, make, act):
         src, dst, sent, got, to, when = make()
@@ -305,13 +319,21 @@
         self.start(lambda: (src, dst, sent, got, to, when))
 
     def wait(self, dst, got, to):
-        self.copy(dst, dst, 0, got, to).wait_recv()
-
-    def finish(self):
-        for make in self.sends:
+        self.copy(dst, dst, None, got, to).wait_recv()
+
+    def finish(self, count=None):
+        count = len(self.sends) if count is None else count
+        for make in self.sends[:count]:
             sent = make()[2]
-            if not (isinstance(sent, int) and sent in self.dropped):
+            if not (isinstance(sent.offset, int) and (sent.key, sent.offset) in self.dropped):
                 self.each(make, lambda copy: copy.wait_send())
+        self.sends = self.sends[count:]
+
+    def reuse(self, count, keep):
+        self.finish(count)
+        assert self.sent_at["next"] <= self.send_sem.shape[0]
+        held = {key: self.sent_at[key] for key in keep}
+        self.sent_at = dict(held, next=max(held[key] + self.counts[key] for key in keep))
 
 
 def where_am_i():
@@ -344,20 +366,27 @@
 
 
 def layer_kernel(
-    tok_in, cot_in, mask_in, norm_in, bias_in, qkv_in, wo_in, w1_in, w2_in,
-    block_out, grad_out, sums_out, qv_out, b1_out, qkv_out, wo_out, w1_out, w2_out,
+    tok_raw, cot_raw, valid_in, gain_in, shift_in, qv_in, b1_in, qkv_in, wo_in, w1_in, w2_in,
+    block_out, grad_out, o_up, o_down, o_qkv, o_wo, bias_all, sums_z,
+    tok_in, cot_in, mask_in, norm_in, bias_in,
     tok, cot, mask, norm, bias, qkv, wo, up, down,
     n1, proj, lse, mix, hid, n2, act, slope,
     norm_row, qkv_row, up_row, part, got_part,
-    ga, gmix, gproj, d_up, d_down, d_qkv, d_wo, r_up, r_down, z_up, z_down, f_up, f_down, o_up, o_down,
-    first_qkv, first_wo, second_qkv, second_wo, z_qkv, z_wo, f_qkv, f_wo, o_qkv, o_wo,
+    n1_t, ga, gmix, gproj, d_up, d_down, d_qkv, d_wo, r_up, r_down, z_up, z_down, f_up, f_down,
+    first_qkv, first_wo, second_qkv, second_wo, z_qkv, z_wo, f_qkv, f_wo,
     s_far, s_mid, s_near, g_far, g_mid, g_near, b_far, b_mid, b_near, g_n1,
-    sums, sums_row, sums_got, sums_z, gb1, gbq, gbv, bias_pack, bias_got, bias_all,
+    sums, sums_row, sums_got, sums_own, gb1, gbq, gbv, bias_pack, bias_got, bias_own,
     local_sem, send_sem, recv_sem,
 ):
     y, x, c, z = where_am_i()
     r = y * 2 + x
     links = Links(send_sem, recv_sem)
+    early = links.base("rdown", 4)
+    early.place(links.sent_at)
+    for j in range(2):
+        tok[j * Q + SENT : j * Q + Q, :] = jnp.zeros((Q - SENT, 1024), BF)
+        for qq in range(4):
+            cot[qq * HALF + j * Q + SENT : qq * HALF + j * Q + Q, :] = jnp.zeros((Q - SENT, 1024), BF)
     me = place(y, x, c, z)
     to_c, to_x, to_y = place(y, x, 1 - c, z), place(y, 1 - x, c, z), place(1 - y, x, c, z)
     greet(y, x, c, z)
@@ -377,13 +406,43 @@
     qkv_at = lambda rr, o, cs: qkv.at[at_rows(rr * 256 + cs * 128, 128, 128), at_rows(o * 384, 384, 128)]
     wo_at = lambda rr, o, cs: wo.at[at_rows(o * 128, 128, 128), at_rows(rr * 256 + cs * 128, 128, 128)]
     s_pc = links.base("pc", 2)
-    links.put(qkv_in.at[:, at_rows((1 - c) * 384, 384, 128)], qkv_at(r, z, c), s_pc, s_pc, to_c)
+    qkv_third = lambda t, cs: qkv_in.at[t, :, at_rows(cs * 128, 128, 128)]
+    qkv_spot = lambda t, cs: qkv.at[at_rows(r * 256 + cs * 128, 128, 128), at_rows(z * 384 + t * 128, 128, 128)]
+    s_pc3 = links.base("pc3", 3)
+    for t in range(3):
+        links.put(qkv_third(t, 1 - c), qkv_spot(t, c), s_pc3 + t, s_pc3 + t, to_c)
     links.put(wo_in.at[at_rows((1 - c) * 128, 128, 128), :], wo_at(r, z, c), s_pc + 1, s_pc + 1, to_c)
-    own_qkv = local(0, qkv_in.at[:, at_rows(c * 384, 384, 128)], qkv_at(r, z, c))
+    own_qkv = [local(at, qkv_third(t, c), qkv_spot(t, c)) for t, at in enumerate((0, 11, 12))]
     own_wo = local(1, wo_in.at[at_rows(c * 128, 128, 128), :], wo_at(r, z, c))
-    own_qkv.start()
+    for one in own_qkv:
+        one.start()
     own_wo.start()
 
+    norm_in[0:2, :] = gain_in[...].astype(F32)
+    norm_in[2:6, :] = shift_in[...].astype(F32)
+    norm_in[6:8, :] = jnp.zeros((2, 128), F32)
+    bias_in[0:2, :] = qv_in[:, at_rows(c * 128, 128, 128)].astype(F32)
+    bias_in[2:4, :] = jnp.where(q == 0, b1_in[0:2, :], jnp.where(q == 1, b1_in[2:4, :], jnp.where(q == 2, b1_in[4:6, :], b1_in[6:8, :]))).astype(F32)
+    bias_in[4:8, :] = jnp.zeros((4, 128), F32)
+    length = valid_in.shape[1]
+    quarter = length // 4
+    source = lax.broadcasted_iota(jnp.int32, (length, FULL), 0)
+    target = lax.broadcasted_iota(jnp.int32, (length, FULL), 1)
+    chosen = None
+    for at in range(4):
+        inside = jnp.logical_and(target >= at * Q, target < at * Q + quarter)
+        match = jnp.logical_and(inside, target - source == at * (Q - quarter))
+        chosen = match if chosen is None else jnp.logical_or(chosen, match)
+    spread = mm((valid_in[...] > 0).astype(F32).astype(BF), chosen.astype(F32).astype(BF), NN)
+    hidden = jnp.where(spread > 0.5, 0.0, MASKED)
+    mask_in[0] = hidden[0:1]
+    mask_in[1] = hidden[1:2]
+    number = tok_raw.shape[0]
+    full_rows = number // 16 * 16
+    for one_raw, one_in in ((tok_raw, tok_in), (cot_raw, cot_in)):
+        for i in range(2):
+            one_in[i, full_rows:Q, :] = jnp.zeros((Q - full_rows, 1024), BF)
+            one_in[i, 0:number, :] = one_raw[:, i, :]
     s_norm, s_bias, s_mask = links.base("norm", 8), links.base("bias", 4), links.base("mask", 1)
     for dd in range(1, 8):
         to = place((y + dd // 4) % 2, (x + (dd // 2) % 2) % 2, (c + dd % 2) % 2, z)
@@ -396,22 +455,23 @@
         one.start()
 
     def move_tokens(key, source, target_at, at):
-        base = links.base(key, 4)
+        base, got = links.base((key, "sent"), 2), links.base((key, "got"), 2)
         target = target_at(z // 2)
         stay = c == z // 2
-        rows = at_rows((z % 2) * Q, Q, 16)
+        rows = at_rows((z % 2) * Q, SENT, 16)
         for i in range(2):
             here = jnp.logical_and(stay, z % 2 == i)
             to = place(y, x, z // 2, 2 * c + i)
             to = (jnp.where(here, place(y, x, 1 - c, z)[0], to[0]), to[1])
-            links.put(source.at[i], target.at[rows], base + i, base + 2 + z % 2, to, jnp.logical_not(here))
+            mine = source.at[i, pl.ds(0, SENT)]
+            links.put(mine, target.at[rows], base + i, got + z % 2, to, jnp.logical_not(here))
 
             @pl.when(here)
-            def _(i=i):
-                local(at, source.at[i], target.at[rows]).start()
+            def _(mine=mine):
+                local(at, mine, target.at[rows]).start()
 
     def wait_tokens(key, source, target_at, at):
-        base = links.base(key, 4)
+        got = links.base((key, "got"), 2)
         target = target_at(c)
         stay = c == z // 2
         for j in range(2):
@@ -419,11 +479,11 @@
 
             @pl.when(here)
             def _(j=j):
-                local(at, source.at[j], target.at[pl.ds(j * Q, Q)]).wait()
+                local(at, source.at[j, pl.ds(0, SENT)], target.at[pl.ds(j * Q, SENT)]).wait()
 
             @pl.when(jnp.logical_not(here))
             def _(j=j):
-                links.wait(target.at[pl.ds(j * Q, Q)], base + 2 + j, to_c)
+                links.wait(target.at[pl.ds(j * Q, SENT)], got + j, to_c)
 
     up_shard = lambda sx, sc: up.at[at_rows(y * 512 + sx * 256 + sc * 128, 128, 128), at_rows(z * 256, 256, 128)]
     down_shard = lambda sx, sc: down.at[at_rows(z * 256, 256, 128), at_rows(y * 512 + sx * 256 + sc * 128, 128, 128)]
@@ -467,8 +527,8 @@
                 links.wait(ref, self.got[n] + o, to_z1)
 
         def begin(self):
+            self.push(1, z, to_z1)
             self.push(0, z, to_z2)
-            self.push(1, z, to_z1)
             self.arrived(z)
 
         def far(self):
@@ -484,29 +544,77 @@
             self.take(z3)
             self.arrived(z3)
 
+    class Line:
+        def __init__(self, key, piece, arrived):
+            self.piece, self.arrived = piece, arrived
+            self.many = len(piece(0))
+            self.got = [links.base((key, "got", n), 4) for n in range(self.many)]
+            self.sent = [links.base((key, "sent", n), 8) for n in range(self.many)]
+
+        def push(self, upward, o, there):
+            onward = z < 3 if upward else z > 0
+            to = place(y, x, c, jnp.minimum(z + 1, 3) if upward else jnp.maximum(z - 1, 0))
+            to = (jnp.where(onward, to[0], to_c[0]), to[1])
+            for n, ref in enumerate(self.piece(o)):
+                links.put(ref, ref, self.sent[n] + 4 * upward + o, self.got[n] + o, to, jnp.logical_and(there, onward))
+
+        def begin(self):
+            self.push(1, z, z >= 0)
+            self.push(0, z, z >= 0)
+            self.arrived(z, None)
+
+        def step(self, far):
+            for upward in (1, 0):
+                o = z - far if upward else z + far
+                there = o >= 0 if upward else o < 4
+                o = jnp.clip(o, 0, 3)
+
+                @pl.when(there)
+                def _():
+                    for n, ref in enumerate(self.piece(o)):
+                        links.wait(ref, self.got[n] + o, to_z1)
+
+                self.push(upward, o, there)
+                self.arrived(o, there)
+
     attn_at = (qkv_at, wo_at)
+
+    def attn_whole(o):
+        return (
+            qkv.at[at_rows(r * 256, 256, 256), at_rows(o * 384, 384, 128)],
+            wo.at[at_rows(o * 128, 128, 128), at_rows(r * 256, 256, 256)],
+        )
+
     s_first = [links.base(("first", n), 8) for n in range(2)]
     s_own = [links.base(("own", n), 8) for n in range(2)]
     s_fwd = [links.base(("fwd", n), 8) for n in range(2)]
     to_first, to_second = (to_x, to_y), (to_y, to_x)
     r_first, r_second = (r_x, r_y), (r_y, r_x)
 
-    def attn_arrived(o):
+    def attn_arrived(o, there):
         for n, at in enumerate(attn_at):
             for cs in range(2):
                 ref, sem = at(r, o, cs), o * 2 + cs
-                links.put(ref, ref, s_first[n] + sem, s_first[n] + sem, to_first[cs])
+                links.put(ref, ref, s_first[n] + sem, s_first[n] + sem, to_first[cs], there)
         for n, at in enumerate(attn_at):
             for cs in range(2):
                 ref, sem = at(r, o, cs), o * 2 + cs
-                links.put(ref, ref, s_own[n] + sem, s_own[n] + sem, to_second[cs])
-
-    def attn_forward(o):
+                links.put(ref, ref, s_own[n] + sem, s_own[n] + sem, to_second[cs], there)
+
+    def attn_forward(o, there=None):
         for n, at in enumerate(attn_at):
             for cs in range(2):
                 ref, sem = at(r_first[cs], o, cs), o * 2 + cs
-                links.wait(ref, s_first[n] + sem, to_x)
-                links.put(ref, ref, s_fwd[n] + sem, s_fwd[n] + sem, to_second[cs])
+
+                def arrive(n=n, ref=ref, sem=sem):
+                    links.wait(ref, s_first[n] + sem, to_x)
+
+                arrive() if there is None else pl.when(there)(arrive)
+                links.put(ref, ref, s_fwd[n] + sem, s_fwd[n] + sem, to_second[cs], there)
+
+    def attn_forward_far(far):
+        attn_forward(jnp.clip(z - far, 0, 3), z >= far)
+        attn_forward(jnp.clip(z + far, 0, 3), z + far < 4)
 
     def attn_finish():
         for o in range(4):
@@ -516,7 +624,7 @@
                     links.wait(at(r_second[cs], o, cs), s_own[n] + sem, to_x)
                     links.wait(at(r_xy, o, cs), s_fwd[n] + sem, to_x)
 
-    attn_fan = Fan("attn", lambda o: [at(r, o, cs) for at in attn_at for cs in range(2)], attn_arrived)
+    attn_line = Line("attn", lambda o: attn_whole(o), attn_arrived)
     up_at = lambda yy, o: up.at[at_rows(yy * 512, 512, 512), at_rows(o * 256, 256, 256)]
     down_at = lambda yy, o: down.at[at_rows(o * 256, 256, 256), at_rows(yy * 512, 512, 512)]
     s_upy, s_downy = links.base("upy", 4), links.base("downy", 4)
@@ -528,17 +636,35 @@
     down_fan = Fan("downf", lambda o: (down_at(y, o),), across(down_at, s_downy))
 
     lse[...] = jnp.zeros_like(lse)
-    own_qkv.wait()
+    for one in own_qkv:
+        one.wait()
     own_wo.wait()
-    links.wait(qkv_at(r, z, 1 - c), s_pc, to_c)
+    for t in range(3):
+        links.wait(qkv_spot(t, 1 - c), s_pc3 + t, to_c)
     links.wait(wo_at(r, z, 1 - c), s_pc + 1, to_c)
-    attn_fan.begin()
-    attn_fan.far()
+    def spread_start(key, ref):
+        base = links.base(("spread", key), 3)
+        links.start(lambda: (block_at(ref, q), block_at(ref, q), base, base, to_x, None))
+        links.start(lambda: (block_at(ref, q), block_at(ref, q), base + 1, base + 1, to_c, None))
+
+    def spread_forward(key, ref):
+        base = links.base(("spread", key), 3)
+        far = lambda: block_at(ref, 2 * (1 - x) + c)
+        links.wait(far(), base, to_x)
+        links.start(lambda: (far(), far(), base + 2, base + 2, to_c, None))
+
+    def spread_wait_near(key, ref):
+        links.wait(block_at(ref, 2 * x + 1 - c), links.base(("spread", key), 3) + 1, to_c)
+
+    def spread_wait_far(key, ref):
+        links.wait(block_at(ref, 2 * (1 - x) + 1 - c), links.base(("spread", key), 3) + 2, to_c)
+
+    attn_line.begin()
+    attn_line.step(1)
     attn_forward(z)
+    attn_line.step(2)
     move_tokens("tok", tok_in, lambda cc: tok, 5)
-    for dx, dc in ((1, 0), (1, 1), (0, 1)):
-        part_up(dx, dc)
-    attn_fan.pair()
+    move_tokens("cot", cot_in, lambda cc: block_at(cot, 2 * x + cc), 8)
     for one in own_small:
         one.wait()
     for dd in range(1, 8):
@@ -555,17 +681,15 @@
         qkv_row[:, zz * 384 + 256 : zz * 384 + 384] = bias[zz, 1:2]
         up_row[:, zz * 256 : zz * 256 + 128] = bias[zz, 2:3]
         up_row[:, zz * 256 + 128 : zz * 256 + 256] = bias[zz, 3:4]
-    attn_fan.diagonal()
-    attn_forward(z2)
-    attn_forward(z1)
+    attn_forward_far(1)
+    attn_line.step(3)
+    attn_forward_far(2)
+    for dx, dc in ((1, 0), (1, 1), (0, 1)):
+        part_up(dx, dc)
     for dx, dc in ((1, 0), (1, 1), (0, 1)):
         part_down(dx, dc)
     own_up.wait()
     own_down.wait()
-    wait_parts(up_shard, s_up)
-    up_fan.begin()
-    attn_forward(z3)
-
     wait_tokens("tok", tok_in, lambda cc: tok, 5)
 
     @pl.loop(0, HALF // 32)
@@ -577,13 +701,13 @@
     s_n1 = links.base("n1", 1)
     half_at = lambda ref, cc: ref.at[at_rows(cc * HALF, HALF, 64), :]
     links.put(half_at(n1, c), half_at(n1, c), s_n1, s_n1, to_c)
-    up_fan.far()
-    move_tokens("cot", cot_in, lambda cc: block_at(cot, 2 * x + cc), 8)
+    attn_forward_far(3)
+    wait_parts(up_shard, s_up)
+    up_fan.begin()
     wait_parts(down_shard, s_down)
+    down_fan.begin()
     links.wait(half_at(n1, 1 - c), s_n1, to_c)
     attn_finish()
-    up_fan.pair()
-    down_fan.begin()
 
     @pl.loop(0, 6)
     def _(j):
@@ -593,23 +717,6 @@
     lane = lax.broadcasted_iota(jnp.int32, (1, 128), 1)
     first_head = lane < 64
     zero = jnp.zeros((), BF)
-
-    def spread_start(key, ref):
-        base = links.base(("spread", key), 3)
-        links.start(lambda: (block_at(ref, q), block_at(ref, q), base, base, to_x, None))
-        links.start(lambda: (block_at(ref, q), block_at(ref, q), base + 1, base + 1, to_c, None))
-
-    def spread_forward(key, ref):
-        base = links.base(("spread", key), 3)
-        far = lambda: block_at(ref, 2 * (1 - x) + c)
-        links.wait(far(), base, to_x)
-        links.start(lambda: (far(), far(), base + 2, base + 2, to_c, None))
-
-    def spread_wait_near(key, ref):
-        links.wait(block_at(ref, 2 * x + 1 - c), links.base(("spread", key), 3) + 1, to_c)
-
-    def spread_wait_far(key, ref):
-        links.wait(block_at(ref, 2 * (1 - x) + 1 - c), links.base(("spread", key), 3) + 2, to_c)
 
     @pl.loop(0, 4)
     def _(zz):
@@ -634,16 +741,12 @@
 
         @pl.when(zz == 0)
         def _():
-            up_fan.diagonal()
-
-        @pl.when(zz == 2)
-        def _():
-            down_fan.far()
-
-        @pl.when(zz == 3)
-        def _():
             wait_tokens("cot", cot_in, lambda cc: block_at(cot, 2 * x + cc), 8)
             spread_start("cot", cot)
+
+        @pl.when(zz == 1)
+        def _():
+            up_fan.pair()
 
     s_part = links.base("part", 1)
 
@@ -667,33 +770,41 @@
         n2[block_rows(q, i * 32, 32), :] = (unit * norm_row[1:2] + norm_row[3:4]).astype(BF)
 
     spread_start("n2", n2)
+    up_fan.far()
     down_fan.pair()
     spread_forward("cot", cot)
     spread_wait_near("cot", cot)
-    for o in range(4):
+
+    def expand(o, start, blocks):
+        columns = at_rows(o * 256, 256, 256)
+
+        @pl.loop(0, blocks)
+        def _(i):
+            rows = at_rows(start + i * Q, Q, 32)
+            v = mm(n2[rows, :], up[:, columns], NN) + up_row[:, columns]
+            value, grade = gelu_both(v)
+            act[rows, columns] = value.astype(BF)
+            slope[rows, columns] = grade.astype(BF)
+
+    n1_t[...] = n1[...].T
+    spread_wait_near("n2", n2)
+    for at, o in enumerate((z, z1, z2, z3)):
         links.wait(up_at(1 - y, o), s_upy + o, to_y)
-
-    def expand(t):
-        @pl.loop(0, 4)
-        def _(j):
-            columns = at_rows(j * 256, 256, 256)
-            for rb in range(2):
-                rows = block_rows(t, rb * Q, Q)
-                v = mm(n2[rows, :], up[:, columns], NN) + up_row[:, columns]
-                value, grade = gelu_both(v)
-                act[rows, columns] = value.astype(BF)
-                slope[rows, columns] = grade.astype(BF)
-
-    expand(q)
-    spread_wait_near("n2", n2)
-    expand(2 * x + 1 - c)
+        expand(o, 2 * x * HALF, 4)
+        if at == 0:
+            up_fan.diagonal()
+        if at == 2:
+            down_fan.far()
+    spread_forward("n2", n2)
+    for at, o in enumerate((z, z1, z2, z3)):
+        expand(o, (2 * (1 - x) + c) * HALF, 2)
     down_fan.diagonal()
-    spread_forward("n2", n2)
-    expand(2 * (1 - x) + c)
     spread_wait_far("n2", n2)
-    expand(2 * (1 - x) + 1 - c)
+    for o in (z, z1, z2, z3):
+        expand(o, (2 * (1 - x) + 1 - c) * HALF, 2)
     spread_wait_far("cot", cot)
 
+    forward_sends = len(links.sends)
     near_other, far_own, far_other = 2 * x + 1 - c, 2 * (1 - x) + c, 2 * (1 - x) + 1 - c
     sums[...] = jnp.zeros_like(sums)
     gb1[...] = jnp.zeros_like(gb1)
@@ -739,11 +850,12 @@
     r_up_at = lambda o: r_up.at[:, at_rows(o * 256, 256, 256)]
 
     def accumulate(target, *sources):
-        count = target.shape[0] // 64
+        step = 64 if target.shape[0] % 64 == 0 else 32
+        count = target.shape[0] // step
 
         @pl.loop(0, count)
         def _(i):
-            rows = at_rows(i * 64, 64, 64)
+            rows = at_rows(i * step, step, step)
             total = target[rows, :].astype(F32)
             for source in sources:
                 total = total + source[rows, :].astype(F32)
@@ -812,6 +924,7 @@
         give_down(o)
     for o in range(4):
         links.wait(down_at(1 - y, o), s_downy + o, to_y)
+    links.reuse(forward_sends, ("rdown",))
 
     s_gfar, s_gmid, s_gnear = links.base("gfar", 1), links.base("gmid", 1), links.base("gnear", 1)
     s_bfar, s_bmid, s_bnear = links.base("bfar", 1), links.base("bmid", 1), links.base("bnear", 1)
@@ -819,22 +932,39 @@
     back_part(far_other, s_far)
     links.put(s_far, g_far, s_gfar, s_gfar, to_c)
     through_slope(far_own)
-    links.copy(part, got_part, s_part, s_part, to_c).wait_send()
-    links.drop(s_part)
     back_part(far_own, part)
     links.wait(g_far, s_gfar, to_c)
     add_rows(s_mid, part, g_far)
     links.put(s_mid, g_mid, s_gmid, s_gmid, to_x)
+    half_down.pair_far()
     through_slope(near_other)
     back_part(near_other, s_near)
     links.put(s_near, g_near, s_gnear, s_gnear, to_c)
+    half_down.pair_near()
     through_slope(q)
     back_part(q, part)
-    half_down.pair_far()
-    half_down.pair_near()
-    for o in z_order:
-        give_up(o)
+    def down_part(t, target, base=None):
+        @pl.loop(0, 4)
+        def _(j):
+            columns = at_rows(j * 256, 256, 256)
+            v = mm(act[block_rows(t, 0, HALF), :], down[:, columns], NN)
+            target[:, columns] = (v if base is None else v + base[:, columns]).astype(target.dtype)
+
+    links.copy(s_far, g_far, s_gfar, s_gfar, to_c).wait_send()
+    links.drop(s_gfar)
+    down_part(far_other, s_far)
+    links.put(s_far, b_far, s_bfar, s_bfar, to_c)
+    down_part(far_own, got_part)
     half_down.far()
+    give_up(z3)
+    give_up(z1)
+    links.wait(b_far, s_bfar, to_c)
+    links.copy(s_mid, g_mid, s_gmid, s_gmid, to_x).wait_send()
+    links.drop(s_gmid)
+    add_rows(s_mid, got_part, b_far)
+    links.put(s_mid, b_mid, s_bmid, s_bmid, to_x)
+    give_up(z2)
+    give_up(z)
 
     links.wait(g_near, s_gnear, to_c)
     links.wait(g_mid, s_gmid, to_x)
@@ -862,20 +992,12 @@
     s_ga = links.base("ga", 1)
     links.put(half_at(ga, c), half_at(ga, c), s_ga, s_ga, to_c)
 
-    def down_part(t, target, base=None):
-        @pl.loop(0, 4)
-        def _(j):
-            columns = at_rows(j * 256, 256, 256)
-            v = mm(act[block_rows(t, 0, HALF), :], down[:, columns], NN)
-            target[:, columns] = (v if base is None else v + base[:, columns]).astype(target.dtype)
-
-    links.copy(s_far, g_far, s_gfar, s_gfar, to_c).wait_send()
-    links.copy(s_mid, g_mid, s_gmid, s_gmid, to_x).wait_send()
     links.copy(s_near, g_near, s_gnear, s_gnear, to_c).wait_send()
-    links.drop(s_gfar, s_gmid, s_gnear)
-    down_part(far_other, s_far)
-    links.put(s_far, b_far, s_bfar, s_bfar, to_c)
-
+    links.drop(s_gnear)
+    down_part(near_other, s_near)
+    links.put(s_near, b_near, s_bnear, s_bnear, to_c)
+    down_part(q, hid, hid)
+    half_up.pair_far()
     links.wait(half_at(ga, 1 - c), s_ga, to_c)
 
     @pl.loop(0, 2)
@@ -888,57 +1010,69 @@
         columns = at_rows(j * 256, 256, 256)
         d_wo[columns, :] = mm(mix[:, columns], ga[...], TN).astype(BF)
 
-    d_qkv_at = lambda rr, o, cs: d_qkv.at[at_rows(rr * 256 + cs * 128, 128, 128), at_rows(o * 384, 384, 128)]
-    d_wo_at = lambda rr, o, cs: d_wo.at[at_rows(o * 128, 128, 128), at_rows(rr * 256 + cs * 128, 128, 128)]
-    d_qkv_all = lambda o: d_qkv.at[at_rows(r * 256, 256, 256), at_rows(o * 384, 384, 128)]
-    d_wo_all = lambda o: d_wo.at[at_rows(o * 128, 128, 128), at_rows(r * 256, 256, 128)]
+    d_qkv_at = lambda rr, o, start, size: d_qkv.at[at_rows(rr * 256 + start, size, 32), at_rows(o * 384, 384, 128)]
+    d_wo_at = lambda rr, o, start, size: d_wo.at[at_rows(o * 128, 128, 128), at_rows(rr * 256 + start, size, 128)]
 
     class Reduce(Fold):
-        def __init__(self, key, at, whole, first, second, over_z, final):
-            super().__init__(key, whole, over_z, final)
-            self.at, self.first, self.second = at, first, second
-            self.s1 = [links.base((key, "first", i), 8) for i in range(2)]
-            self.s2 = links.base((key, "second"), 8)
-
-        def begin(self, o, cs):
-            sem = 2 * o + cs
-            for i, rr in ((1, r_xy), (0, r_first[cs])):
-                links.start(
-                    lambda i=i, rr=rr: (
-                        self.at(rr, o, cs), self.first.at[i, o, cs], self.s1[i] + sem, self.s1[i] + sem, to_first[cs], None,
-                    )
-                )
-
-        def middle(self, o, cs):
-            sem = 2 * o + cs
-            links.wait(self.first.at[1, o, cs], self.s1[1] + sem, to_x)
-            accumulate(self.at(r_second[cs], o, cs), self.first.at[1, o, cs])
-            links.start(
-                lambda: (
-                    self.at(r_second[cs], o, cs), self.second.at[o, cs], self.s2 + sem, self.s2 + sem, to_second[cs], None,
-                )
-            )
+        def __init__(self, key, at, parts, first, second, over_z, final):
+            super().__init__(key, lambda o: at(r, o, 0, parts[-1][0] + parts[-1][1]), over_z, final)
+            self.at, self.parts, self.first, self.second = at, parts, first, second
+            self.s1 = [links.base((key, "first", i), 4 * len(parts)) for i in range(2)]
+            self.s2 = links.base((key, "second"), 4 * len(parts))
+
+        def block(self, rr, o, p):
+            return self.at(rr, o, self.parts[p][0], self.parts[p][1])
+
+        def spot(self, ref, p):
+            return cut_of(self, ref, self.parts[p][0], self.parts[p][1])
+
+        def make(self, o, p, i):
+            way = self.parts[p][2]
+            rr, sem = (r_first[way] if i == 0 else r_xy), self.s1[i] + (len(self.parts) * o + p)
+            return self.block(rr, o, p), self.spot(self.first.at[i, o], p), sem, sem, to_first[way], None
+
+        def offer(self, o):
+            for p in range(len(self.parts)):
+                for i in (1, 0):
+                    links.each(functools.partial(self.make, o, p, i), lambda copy: copy.start())
+
+        def promised(self):
+            for o in range(4):
+                for p in range(len(self.parts)):
+                    for i in range(2):
+                        links.sends.append(functools.partial(self.make, o, p, i))
+
+        def middle(self, o):
+            for p in range(len(self.parts)):
+                way = self.parts[p][2]
+                got = self.spot(self.first.at[1, o], p)
+                links.wait(got, self.s1[1] + (len(self.parts) * o + p), to_x)
+                accumulate(self.block(r_second[way], o, p), got)
+
+                def make(p=p, way=way):
+                    sem = self.s2 + (len(self.parts) * o + p)
+                    return self.block(r_second[way], o, p), self.spot(self.second.at[o], p), sem, sem, to_second[way], None
+
+                links.start(make)
 
         def collect(self, o):
-            for cs in range(2):
-                sem = 2 * o + cs
-                links.wait(self.first.at[0, o, cs], self.s1[0] + sem, to_x)
-                links.wait(self.second.at[o, cs], self.s2 + sem, to_x)
-                accumulate(self.at(r, o, cs), self.first.at[0, o, cs], self.second.at[o, cs])
-
-    red_wo = Reduce("red_wo", d_wo_at, d_wo_all, first_wo, second_wo, z_wo, f_wo)
-    red_qkv = Reduce("red_qkv", d_qkv_at, d_qkv_all, first_qkv, second_qkv, z_qkv, f_qkv)
-    for cs in range(2):
-        for o in z_order:
-            red_wo.begin(o, cs)
-
-    down_part(far_own, part)
-    links.wait(b_far, s_bfar, to_c)
-    add_rows(s_mid, part, b_far)
-    links.put(s_mid, b_mid, s_bmid, s_bmid, to_x)
-    down_part(near_other, s_near)
-    links.put(s_near, b_near, s_bnear, s_bnear, to_c)
-    down_part(q, hid, hid)
+            for p in range(len(self.parts)):
+                links.wait(self.spot(self.first.at[0, o], p), self.s1[0] + (len(self.parts) * o + p), to_x)
+                links.wait(self.spot(self.second.at[o], p), self.s2 + (len(self.parts) * o + p), to_x)
+            accumulate(self.piece(o), self.first.at[0, o], self.second.at[o])
+
+    def cut_of(owner, ref, start, size):
+        return ref.at[pl.ds(start, size), :] if owner.by_rows else ref.at[:, pl.ds(start, size)]
+
+    Reduce.by_rows = True
+    red_wo = Reduce("red_wo", d_wo_at, ((0, 256, 0),), first_wo, second_wo, z_wo, f_wo)
+    red_wo.by_rows = False
+    red_qkv = Reduce("red_qkv", d_qkv_at, ((0, 160, 0), (160, 96, 1)), first_qkv, second_qkv, z_qkv, f_qkv)
+    for o in z_order:
+        red_wo.offer(o)
+    red_wo.promised()
+
+    half_up.pair_near()
 
     s_oup, s_odown = links.base("oup", 4), links.base("odown", 4)
 
@@ -960,8 +1094,58 @@
 
             links.start(make)
 
+    def send_home(key, source, target, at):
+        base, got = links.base((key, "sent"), 2), links.base((key, "got"), 2)
+        for j in range(2):
+            def make(j=j):
+                here = jnp.logical_and(z // 2 == c, z == 2 * c + j)
+                to = place(y, x, z // 2, 2 * c + j)
+                to = (jnp.where(here, place(y, x, 1 - c, z)[0], to[0]), to[1])
+                return source.at[pl.ds(j * Q, SENT)], target.at[z % 2, pl.ds(0, SENT)], base + j, got + z % 2, to, jnp.logical_not(here)
+
+            links.start(make)
+
+            @pl.when(jnp.logical_and(z // 2 == c, z == 2 * c + j))
+            def _(j=j):
+                local(at, source.at[pl.ds(j * Q, SENT)], target.at[z % 2, pl.ds(0, SENT)]).start()
+
+    def wait_home(key, source, target, at):
+        got = links.base((key, "got"), 2)
+        for i in range(2):
+            here = jnp.logical_and(z // 2 == c, z % 2 == i)
+
+            @pl.when(here)
+            def _(i=i):
+                local(at, source.at[pl.ds(0, SENT)], target.at[i, pl.ds(0, SENT)]).wait()
+
+            @pl.when(jnp.logical_not(here))
+            def _(i=i):
+                links.wait(target.at[i, pl.ds(0, SENT)], got + i, to_c)
+
+    def finish_block():
+        links.wait(b_near, s_bnear, to_c)
+        links.wait(b_mid, s_bmid, to_x)
+        links.copy(s_near, b_near, s_bnear, s_bnear, to_c).wait_send()
+
+        @pl.loop(0, HALF // 32)
+        def _(i):
+            rows = at_rows(i * 32, 32, 32)
+            total = hid[rows, :] + b_near[rows, :].astype(F32) + b_mid[rows, :].astype(F32) + norm_row[5:6]
+            s_near[rows, :] = total.astype(BF)
+
+        send_home("block", s_near, block_out, 9)
+
+    links.drop(s_bnear)
+
+    kept = []
+
+    def keep(at, source, target):
+        kept.append(local(at, source, target))
+        kept[-1].start()
+
     @pl.loop(0, 4)
-    def _(zz):
+    def _(kk):
+        zz = 2 * ((z // 2 + 1 - kk % 2) % 2) + (z % 2 + 1 - kk // 2) % 2
         base = zz * 384
         keys = proj[:, at_rows(base + 128, 128, 128)]
         values = proj[:, at_rows(base + 256, 128, 128)]
@@ -996,72 +1180,44 @@
         gbq[:, at_rows(zz * 128, 128, 128)] = sum_queries
         gbv[:, at_rows(zz * 128, 128, 128)] = jnp.sum(d_values.reshape(FULL // 8, 8, 128), axis=0)
 
-        @pl.when(zz == 0)
+        columns = at_rows(base, 384, 128)
+        for rr in range(4):
+            rows = pl.ds(rr * 256, 256)
+            d_qkv[rows, columns] = mm(n1_t[rows, :], gproj[:, columns], NN).astype(BF)
+        red_qkv.offer(zz)
+
+        @pl.when(kk == 0)
         def _():
-            half_down.last()
-            scatter_down()
-
-        @pl.when(zz == 1)
-        def _():
-            half_up.pair_far()
-            half_up.pair_near()
-
-        @pl.when(zz == 2)
+            finish_block()
+
+        @pl.when(kk == 1)
         def _():
             half_up.far()
 
-    links.wait(b_near, s_bnear, to_c)
-    links.wait(b_mid, s_bmid, to_x)
-    links.copy(s_far, b_far, s_bfar, s_bfar, to_c).wait_send()
-    links.copy(s_near, b_near, s_bnear, s_bnear, to_c).wait_send()
-    links.drop(s_bfar, s_bnear)
-
-    @pl.loop(0, HALF // 32)
-    def _(i):
-        rows = at_rows(i * 32, 32, 32)
-        total = hid[rows, :] + b_near[rows, :].astype(F32) + b_mid[rows, :].astype(F32) + norm_row[5:6]
-        s_near[rows, :] = total.astype(BF)
-
-    def send_home(key, source, target, at):
-        base = links.base(key, 4)
-        for j in range(2):
-            def make(j=j):
-                here = jnp.logical_and(z // 2 == c, z == 2 * c + j)
-                to = place(y, x, z // 2, 2 * c + j)
-                to = (jnp.where(here, place(y, x, 1 - c, z)[0], to[0]), to[1])
-                return source.at[pl.ds(j * Q, Q)], target.at[z % 2], base + j, base + 2 + z % 2, to, jnp.logical_not(here)
-
-            links.start(make)
-
-            @pl.when(jnp.logical_and(z // 2 == c, z == 2 * c + j))
-            def _(j=j):
-                local(at, source.at[pl.ds(j * Q, Q)], target.at[z % 2]).start()
-
-    def wait_home(key, source, target, at):
-        base = links.base(key, 4)
-        for i in range(2):
-            here = jnp.logical_and(z // 2 == c, z % 2 == i)
-
-            @pl.when(here)
-            def _(i=i):
-                local(at, source.at[pl.ds(0, Q)], target.at[i]).wait()
-
-            @pl.when(jnp.logical_not(here))
-            def _(i=i):
-                links.wait(target.at[i], base + 2 + i, to_c)
-
-    send_home("block", s_near, block_out, 9)
-
-    def weigh(rr):
-        d_qkv[at_rows(rr * 256, 256, 256), :] = mm(n1[:, at_rows(rr * 256, 256, 256)], gproj[...], TN).astype(BF)
-
-    weigh(r_xy)
-    weigh(r_x)
-    for o in z_order:
-        red_qkv.begin(o, 0)
-    weigh(r_y)
-    for o in z_order:
-        red_qkv.begin(o, 1)
+        @pl.when(kk == 2)
+        def _():
+            red_qkv.middle(z3)
+
+        @pl.when(kk == 3)
+        def _():
+            for o in z_order:
+                red_wo.middle(o)
+
+    red_qkv.promised()
+    for zz in range(4):
+        flat = lambda ref, start: jnp.sum(ref[:, start : start + 128], axis=0, keepdims=True)
+        bias_pack[zz, 0:1] = flat(gbq, zz * 128)
+        bias_pack[zz, 1:2] = flat(gbv, zz * 128)
+        bias_pack[zz, 2:3] = flat(gb1, zz * 256)
+        bias_pack[zz, 3:4] = flat(gb1, zz * 256 + 128)
+        bias_pack[zz, 4:8] = jnp.zeros((4, 128), F32)
+    s_bz, s_ball = links.base("bz", 4), links.base("ball", 8)
+    for dz in range(1, 4):
+        def make(dz=dz):
+            tz = (z + dz) % 4
+            return bias_pack.at[tz], bias_got.at[dz], s_bz + dz, s_bz + dz, place(y, x, c, tz), None
+
+        links.start(make)
 
     def front_part(cc, target):
         @pl.loop(0, 4)
@@ -1070,13 +1226,14 @@
             target[:, columns] = mm(gproj[at_rows(cc * HALF, HALF, 64), :], qkv[columns, :], NT).astype(target.dtype)
 
     s_gn1 = links.base("gn1", 1)
+    links.copy(s_far, b_far, s_bfar, s_bfar, to_c).wait_send()
+    links.drop(s_bfar)
     front_part(1 - c, s_far)
     links.put(s_far, g_n1, s_gn1, s_gn1, to_c)
-    for o in z_order:
-        for cs in range(2):
-            red_wo.middle(o, cs)
-    weigh(r)
     front_part(c, part)
+    for o in (z1, z2):
+        red_qkv.middle(o)
+    red_qkv.pair_far()
     links.wait(g_n1, s_gn1, to_c)
     links.copy(s_mid, b_mid, s_bmid, s_bmid, to_x).wait_send()
     links.drop(s_bmid)
@@ -1096,54 +1253,39 @@
         tally(2, grad)
         s_mid[rows, :] = (got_part[rows, :] + moved).astype(BF)
 
-    send_home("home", s_mid, grad_out, 10)
-
     for row in range(6):
         sums_row[row : row + 1, :] = jnp.sum(sums[row * 8 : row * 8 + 8, :], axis=0, keepdims=True)
     sums_row[6:8, :] = jnp.zeros((2, 1024), F32)
     for dd in range(8):
         norm[dd] = sums_row[:, dd * 128 : dd * 128 + 128]
-    s_sum, s_sumz = links.base("sum", 8), links.base("sumz", 8)
+    s_sum, s_sumz = links.base("sum", 8), links.base("sumz", 4)
     for dd in range(1, 8):
         def make(dd=dd):
             ty, tx, tc = (y + dd // 4) % 2, (x + (dd // 2) % 2) % 2, (c + dd % 2) % 2
             return norm.at[4 * ty + 2 * tx + tc], sums_got.at[dd], s_sum + dd, s_sum + dd, place(ty, tx, tc, z), None
 
         links.start(make)
-    for zz in range(4):
-        flat = lambda ref, start: jnp.sum(ref[:, start : start + 128], axis=0, keepdims=True)
-        bias_pack[zz, 0:1] = flat(gbq, zz * 128)
-        bias_pack[zz, 1:2] = flat(gbv, zz * 128)
-        bias_pack[zz, 2:3] = flat(gb1, zz * 256)
-        bias_pack[zz, 3:4] = flat(gb1, zz * 256 + 128)
-        bias_pack[zz, 4:8] = jnp.zeros((4, 128), F32)
-    s_bz, s_ball = links.base("bz", 4), links.base("ball", 8)
-    for dz in range(1, 4):
-        def make(dz=dz):
-            tz = (z + dz) % 4
-            return bias_pack.at[tz], bias_got.at[dz], s_bz + dz, s_bz + dz, place(y, x, c, tz), None
-
-        links.start(make)
-
+    send_home("home", s_mid, grad_out, 10)
+    red_qkv.pair_near()
+    red_qkv.middle(z)
+    red_qkv.far()
+    red_wo.pair_far()
+    red_wo.pair_near()
+    red_wo.far()
+    half_down.last()
+    scatter_down()
+    keep(17, f_down.at[:, at_rows(q * 128, 128, 128)], o_down.at[q])
     half_up.last()
     scatter_up()
-    red_wo.pair_far()
-    red_wo.pair_near()
-    for o in z_order:
-        for cs in range(2):
-            red_qkv.middle(o, cs)
-    red_wo.far()
-    red_qkv.pair_far()
-    red_qkv.pair_near()
-    red_qkv.far()
-
+    keep(18, f_up.at[at_rows(q * 128, 128, 128), :], o_up.at[q])
     for dz in range(1, 4):
         links.wait(bias_got.at[dz], s_bz + dz, to_c)
-    bias_all[d] = bias_pack[z] + bias_got[1] + bias_got[2] + bias_got[3]
+    bias_own[...] = bias_pack[z] + bias_got[1] + bias_got[2] + bias_got[3]
+    keep(13, bias_own, bias_all.at[d])
     for dd in range(1, 8):
         def make(dd=dd):
             to = place((y + dd // 4) % 2, (x + (dd // 2) % 2) % 2, (c + dd % 2) % 2, z)
-            return bias_all.at[d], bias_all.at[d], s_ball + dd, s_ball + dd, to, None
+            return bias_own, bias_all.at[d], s_ball + dd, s_ball + dd, to, None
 
         links.start(make)
     for dd in range(1, 8):
@@ -1151,118 +1293,128 @@
     total = norm[d]
     for dd in range(1, 8):
         total = total + sums_got[dd]
-    sums_z[0] = total
+    sums_own[...] = total
+    keep(14, sums_own, sums_z.at[0])
     for dz in range(1, 4):
         def make(dz=dz):
-            return sums_z.at[0], sums_z.at[dz], s_sumz + dz, s_sumz + dz, place(y, x, c, (z + dz) % 4), None
+            return sums_own, sums_z.at[dz], s_sumz + dz, s_sumz + dz, place(y, x, c, (z + dz) % 4), None
 
         links.start(make)
-
     red_wo.last()
-
-    w1_out[:, at_rows(q * 256, 256, 256)] = f_up[at_rows(q * 128, 128, 128), :].astype(F32)
-    w2_out[at_rows(q * 256, 256, 256), :] = f_down[:, at_rows(q * 128, 128, 128)].astype(F32)
+    s_owo = links.base("owo", 1)
+    links.put(f_wo.at[:, at_rows((1 - c) * 128, 128, 128)], o_wo.at[c], s_owo, s_owo, to_c)
+    keep(16, f_wo.at[:, at_rows(c * 128, 128, 128)], o_wo.at[c])
+
     for dx, dc in ((1, 0), (1, 1), (0, 1)):
         rel, source = 2 * dx + dc, 2 * ((x + dx) % 2) + (c + dc) % 2
         links.wait(o_up.at[source], s_oup + rel, to_c)
         links.wait(o_down.at[source], s_odown + rel, to_c)
-        w1_out[:, at_rows(source * 256, 256, 256)] = o_up[source].astype(F32)
-        w2_out[at_rows(source * 256, 256, 256), :] = o_down[source].astype(F32)
 
     for dd in range(1, 8):
         source = 4 * ((y + dd // 4) % 2) + 2 * ((x + (dd // 2) % 2) % 2) + (c + dd % 2) % 2
         links.wait(bias_all.at[source], s_ball + dd, to_c)
-    for cc in range(2):
-        together = bias_all[cc] + bias_all[2 + cc] + bias_all[4 + cc] + bias_all[6 + cc]
-        qv_out[:, cc * 128 : cc * 128 + 128] = together[0:2]
-    for qq in range(4):
-        together = bias_all[qq] + bias_all[4 + qq]
-        b1_out[qq * 2 : qq * 2 + 2, :] = together[2:4]
     for dz in range(1, 4):
         links.wait(sums_z.at[dz], s_sumz + dz, to_c)
-    sums_out[...] = sums_z[0] + sums_z[1] + sums_z[2] + sums_z[3]
 
     red_qkv.last()
     s_oqkv, s_owo = links.base("oqkv", 1), links.base("owo", 1)
-    links.put(f_qkv.at[at_rows((1 - c) * 128, 128, 128), :], o_qkv, s_oqkv, s_oqkv, to_c)
-    links.put(f_wo.at[:, at_rows((1 - c) * 128, 128, 128)], o_wo, s_owo, s_owo, to_c)
-    qkv_out[:, at_rows(c * 384, 384, 128)] = f_qkv[at_rows(c * 128, 128, 128), :].astype(F32)
-    wo_out[at_rows(c * 128, 128, 128), :] = f_wo[:, at_rows(c * 128, 128, 128)].astype(F32)
-    links.wait(o_qkv, s_oqkv, to_c)
-    links.wait(o_wo, s_owo, to_c)
-    qkv_out[:, at_rows((1 - c) * 384, 384, 128)] = o_qkv[...].astype(F32)
-    wo_out[at_rows((1 - c) * 128, 128, 128), :] = o_wo[...].astype(F32)
+    links.put(f_qkv.at[at_rows((1 - c) * 128, 128, 128), :], o_qkv.at[c], s_oqkv, s_oqkv, to_c)
+    keep(15, f_qkv.at[at_rows(c * 128, 128, 128), :], o_qkv.at[c])
+    links.wait(o_qkv.at[1 - c], s_oqkv, to_c)
+    links.wait(o_wo.at[1 - c], s_owo, to_c)
     wait_home("block", s_near, block_out, 9)
     wait_home("home", s_mid, grad_out, 10)
+    for one in kept:
+        one.wait()
     links.finish()
-
-
-def prepare(inputs, valid_mask, cotangent, ln_gain, d_bias, w_qkv, b_qv, b_1):
-    y, x, c, z = where_am_i()
-    rows = inputs.shape[0]
-    turn = lambda v: jnp.pad(jnp.transpose(v, (1, 0, 2)), ((0, 0), (0, Q - rows), (0, 0)))
-    mask = jnp.where(valid_mask.reshape(2, 4, rows) > 0, 0.0, MASKED).astype(F32)
-    mask = jnp.pad(mask, ((0, 0), (0, 0), (0, Q - rows)), constant_values=MASKED).reshape(2, 1, FULL)
-    norm = jnp.pad(jnp.concatenate([ln_gain, d_bias]).astype(F32), ((0, 2), (0, 0)))
-    bias = jnp.concatenate(
-        [
-            lax.dynamic_slice(b_qv, (0, c * 128), (2, 128)),
-            lax.dynamic_slice(b_1, ((2 * x + c) * 256,), (256,)).reshape(2, 128),
-        ]
-    ).astype(F32)
-    bias = jnp.pad(bias, ((0, 4), (0, 0)))
-    qkv = jnp.transpose(w_qkv.reshape(128, 3, 2, 128), (0, 2, 1, 3)).reshape(128, 768)
-    return turn(inputs), turn(cotangent), mask, norm, bias, qkv
+    assert links.got_at["next"] <= recv_sem.shape[0]
+    assert links.sent_at["next"] <= send_sem.shape[0]
 
 
 def layer_call(*operands):
     shape = jax.ShapeDtypeStruct
     hbm, vmem = pl.BlockSpec(memory_space=pl.ANY), pl.BlockSpec(memory_space=pltpu.VMEM)
     outs = [
-        shape((2, Q, 1024), BF), shape((2, Q, 1024), BF), shape((8, 128), F32), shape((2, 256), F32),
-        shape((8, 128), F32), shape((128, 768), F32), shape((256, 128), F32), shape((128, 1024), F32),
-        shape((1024, 128), F32),
+        shape((2, Q, 1024), BF), shape((2, Q, 1024), BF), shape((4, 128, 256), BF), shape((4, 256, 128), BF),
+        shape((2, 128, 384), BF), shape((2, 128, 128), BF), shape((8, 8, 128), F32), shape((4, 8, 128), F32),
     ]
     low = lambda *dims: pltpu.VMEM(dims, BF)
     wide = lambda *dims: pltpu.VMEM(dims, F32)
     scratch = [
+        low(2, Q, 1024), low(2, Q, 1024), wide(2, 1, FULL), wide(8, 128), wide(8, 128),
         low(HALF, 1024), low(4 * HALF, 1024), wide(2, 2, 1, FULL), wide(8, 8, 128), wide(4, 8, 128),
         low(1024, 1536), low(512, 1024), low(1024, 1024), low(1024, 1024),
         low(FULL, 1024), low(FULL, 1536), wide(FULL, 128), low(FULL, 512), wide(HALF, 1024),
         low(4 * HALF, 1024), low(4 * HALF, 1024), low(4 * HALF, 1024),
         wide(8, 1024), wide(1, 1536), wide(1, 1024), wide(HALF, 1024), wide(HALF, 1024),
-        low(FULL, 1024), low(FULL, 512), low(FULL, 1536),
+        low(1024, FULL), low(FULL, 1024), low(FULL, 512), low(FULL, 1536),
         low(1024, 1024), low(1024, 1024), low(1024, 1536), low(512, 1024),
         low(512, 1024), low(1024, 512), low(3, 512, 256), low(3, 256, 512),
-        low(512, 256), low(256, 512), low(4, 128, 256), low(4, 256, 128),
-        low(2, 4, 2, 128, 384), low(2, 4, 2, 128, 128), low(4, 2, 128, 384), low(4, 2, 128, 128),
-        low(3, 256, 384), low(3, 128, 256), low(256, 384), low(128, 256), low(128, 384), low(128, 128),
+        low(512, 256), low(256, 512),
+        low(2, 4, 256, 384), low(2, 4, 128, 256), low(4, 256, 384), low(4, 128, 256),
+        low(3, 256, 384), low(3, 128, 256), low(256, 384), low(128, 256),
         *[low(HALF, 1024)] * 10,
-        wide(48, 1024), wide(8, 1024), wide(8, 8, 128), wide(4, 8, 128),
-        wide(8, 1024), wide(8, 512), wide(8, 512), wide(4, 8, 128), wide(4, 8, 128), wide(8, 8, 128),
-        pltpu.SemaphoreType.DMA((16,)), pltpu.SemaphoreType.DMA((320,)), pltpu.SemaphoreType.DMA((320,)),
+        wide(48, 1024), wide(8, 1024), wide(8, 8, 128), wide(8, 128),
+        wide(8, 1024), wide(8, 512), wide(8, 512), wide(4, 8, 128), wide(4, 8, 128), wide(8, 128),
+        pltpu.SemaphoreType.DMA((19,)), pltpu.SemaphoreType.DMA((130,)), pltpu.SemaphoreType.DMA((212,)),
     ]
     return pl.pallas_call(
         layer_kernel,
         out_shape=outs,
-        in_specs=[hbm] * 9,
-        out_specs=[hbm, hbm] + [vmem] * 7,
+        in_specs=[vmem] * 7 + [hbm] * 4,
+        out_specs=[hbm] * 8,
         scratch_shapes=scratch,
         compiler_params=pltpu.CompilerParams(collective_id=0, has_side_effects=True, vmem_limit_bytes=67043328),
         name="layer",
     )(*operands)
 
 
+def finish_kernel(
+    block_in, grad_in, up_in, down_in, qkv_in, wo_in, bias_in, sums_in,
+    block, grad, gain, shift, qkv, qv, wo, w1, b1, w2,
+):
+    rows = grad.shape[0]
+    for i in range(2):
+        grad[:, i, :] = grad_in[i, 0:rows, :].astype(F32)
+    block[...] = jnp.stack([block_in[0, 0:rows, :], block_in[1, 0:rows, :]], axis=1)
+    total = sums_in[0] + sums_in[1] + sums_in[2] + sums_in[3]
+    gain[...] = total[0:2]
+    shift[...] = total[2:6]
+    for cc in range(2):
+        lanes = pl.ds(cc * 128, 128)
+        for t in range(3):
+            qkv[t, :, lanes] = qkv_in[cc, :, t * 128 : t * 128 + 128].astype(F32)
+        qv[:, lanes] = (bias_in[cc] + bias_in[2 + cc] + bias_in[4 + cc] + bias_in[6 + cc])[0:2]
+        wo[pl.ds(cc * 128, 128), :] = wo_in[cc].astype(F32)
+    for qq in range(4):
+        w1[:, pl.ds(qq * 256, 256)] = up_in[qq].astype(F32)
+        w2[pl.ds(qq * 256, 256), :] = down_in[qq].astype(F32)
+        b1[pl.ds(qq * 2, 2), :] = (bias_in[qq] + bias_in[4 + qq])[2:4]
+
+
+def finish_call(rows, *parts):
+    shape = jax.ShapeDtypeStruct
+    return pl.pallas_call(
+        finish_kernel,
+        out_shape=[
+            shape((rows, 2, 1024), BF), shape((rows, 2, 1024), F32), shape((2, 128), F32), shape((4, 128), F32),
+            shape((3, 128, 256), F32), shape((2, 256), F32), shape((256, 128), F32), shape((128, 1024), F32),
+            shape((8, 128), F32), shape((1024, 128), F32),
+        ],
+        in_specs=[pl.BlockSpec(memory_space=pltpu.VMEM)] * 8,
+        out_specs=[pl.BlockSpec(memory_space=pltpu.VMEM)] * 10,
+        name="finish",
+    )(*parts)
+
+
 def fast_body(inputs, valid_mask, cotangent, ln_gain, d_bias, w_qkv, b_qv, w_o, w_1, b_1, w_2):
     rows = inputs.shape[0]
-    block, grad, sums, qv, b1, qkv, wo, w1, w2 = layer_call(
-        *prepare(inputs, valid_mask, cotangent, ln_gain, d_bias, w_qkv, b_qv, b_1), w_o, w_1, w_2
-    )
-    back = lambda v: jnp.transpose(v[:, :rows], (1, 0, 2))
-    w_qkv_grad = jnp.transpose(qkv.reshape(128, 2, 3, 128), (0, 2, 1, 3)).reshape(128, 3, 256)
-    return (
-        back(block), back(grad).astype(F32), sums[:2], sums[2:6], w_qkv_grad, qv, wo, w1, b1.reshape(1024), w2,
-    )
+    parts = layer_call(
+        inputs, cotangent, valid_mask, ln_gain, d_bias, b_qv, b_1.reshape(8, 128),
+        jnp.transpose(w_qkv, (1, 0, 2)), w_o, w_1, w_2,
+    )
+    block, grad, gain, shift, qkv, qv, wo, w1, b1, w2 = finish_call(rows, *parts)
+    return block, grad, gain, shift, jnp.transpose(qkv, (1, 0, 2)), qv, wo, w1, b1.reshape(1024), w2
 
 
 def solution(mesh):

time: 244 us -> 212 us (0.87)
  local copies, waits for them, and re-layouts: 17.8 us -> 0 us
  Pallas kernels: 222 us -> 211 us
  other arithmetic: 2.73 us -> 0 us
    pallas_call x1 -> x2, Pallas kernels: 222 us -> 211 us  [the longest x1 207 us: layer_call(): pl.pallas_call(layer_kernel, out_shape=outs, in_specs=[vmem] * 7 + [hbm]...]
    unnamed x29 -> x0, local copies, waits for them, and re-layouts: 9.11 us -> none
    slice x2 -> x0, local copies, waits for them, and re-layouts: 2.6 us -> none  [the longest x1 1.34 us: fast_body(): sums[:2]]
where the time goes in v2:
time: 212 us; the launch traced here: 211 us
  Pallas kernels  211 us (100%)
    pallas_call x1, Pallas kernels, layer_call(): pl.pallas_call(layer_kernel, out_shape=outs, in_specs=[vmem] * 7 + [hbm]...  207 us

profile of v2, /device:TPU:1, one launch (start us, length us, event | category | flops | bytes accessed | tf_op | source)
XLA Modules:
  0.0 211.4 jit_solution(8971803855480587146)
XLA Ops:
  0.6 207.0 %layer.1 = (bf16[2,160,1024]{2,1,0:T(8,128)(2,1)}, bf16[2,160,1024]{2,1,0:T(8,128)(2,1)}, bf16[4,128,256]{2,1,0:T(8,128)(2,1)}, bf16[4,256,128]{2,1,0:T(8,128)(2...) custom-call(bf16[146,2,1024]{2,1,0:T(2,128)(2,1)} %tok_raw.1, ...), custom_call_target="tpu_custom_call" | custom-call | tf_op jit(solution)/shard_map/layer/pallas_call | solution.py:1361
  207.7 3.8 %finish.1 = (bf16[146,2,1024]{2,1,0:T(2,128)(2,1)}, f32[146,2,1024]{2,1,0:T(2,128)}, f32[2,128]{1,0:T(2,128)}, f32[4,128]{1,0:T(4,128)}, f32[3,128,256]{2,1,0:T(...) custom-call(bf16[2,160,1024]{2,1,0:T(8,128)(2,1)} %get-tuple-element, ...), custom_call_target="tpu_custom_call" | custom-call | tf_op jit(solution)/shard_map/finish/pallas_call | solution.py:1397

commit v3 on v2

--- a/solution.py
+++ b/solution.py
@@ -366,9 +366,9 @@
 
 
 def layer_kernel(
-    tok_raw, cot_raw, valid_in, gain_in, shift_in, qv_in, b1_in, qkv_in, wo_in, w1_in, w2_in,
+    tok_src, cot_src, valid_in, gain_in, shift_in, qv_in, b1_in, qkv_in, wo_in, w1_in, w2_in,
     block_out, grad_out, o_up, o_down, o_qkv, o_wo, bias_all, sums_z,
-    tok_in, cot_in, mask_in, norm_in, bias_in,
+    tok_raw, cot_raw, tok_in, cot_in, mask_in, norm_in, bias_in,
     tok, cot, mask, norm, bias, qkv, wo, up, down,
     n1, proj, lse, mix, hid, n2, act, slope,
     norm_row, qkv_row, up_row, part, got_part,
@@ -389,6 +389,12 @@
             cot[qq * HALF + j * Q + SENT : qq * HALF + j * Q + Q, :] = jnp.zeros((Q - SENT, 1024), BF)
     me = place(y, x, c, z)
     to_c, to_x, to_y = place(y, x, 1 - c, z), place(y, 1 - x, c, z), place(1 - y, x, c, z)
+    raw_copies = [
+        pltpu.make_async_copy(source, target, local_sem.at[at])
+        for source, target, at in ((tok_src, tok_raw, 19), (cot_src, cot_raw, 20))
+    ]
+    for one in raw_copies:
+        one.start()
     greet(y, x, c, z)
 
     block_at = lambda ref, t: ref.at[at_rows(t * HALF, HALF, 64), :]
@@ -418,6 +424,212 @@
         one.start()
     own_wo.start()
 
+    def move_tokens(key, source, target_at, at):
+        base, got = links.base((key, "sent"), 2), links.base((key, "got"), 2)
+        target = target_at(z // 2)
+        stay = c == z // 2
+        rows = at_rows((z % 2) * Q, SENT, 16)
+        for i in range(2):
+            here = jnp.logical_and(stay, z % 2 == i)
+            to = place(y, x, z // 2, 2 * c + i)
+            to = (jnp.where(here, place(y, x, 1 - c, z)[0], to[0]), to[1])
+            mine = source.at[i, pl.ds(0, SENT)]
+            links.put(mine, target.at[rows], base + i, got + z % 2, to, jnp.logical_not(here))
+
+            @pl.when(here)
+            def _(mine=mine):
+                local(at, mine, target.at[rows]).start()
+
+    def wait_tokens(key, source, target_at, at):
+        got = links.base((key, "got"), 2)
+        target = target_at(c)
+        stay = c == z // 2
+        for j in range(2):
+            here = jnp.logical_and(stay, z % 2 == j)
+
+            @pl.when(here)
+            def _(j=j):
+                local(at, source.at[j, pl.ds(0, SENT)], target.at[pl.ds(j * Q, SENT)]).wait()
+
+            @pl.when(jnp.logical_not(here))
+            def _(j=j):
+                links.wait(target.at[pl.ds(j * Q, SENT)], got + j, to_c)
+
+    up_shard = lambda sx, sc: up.at[at_rows(y * 512 + sx * 256 + sc * 128, 128, 128), at_rows(z * 256, 256, 128)]
+    down_shard = lambda sx, sc: down.at[at_rows(z * 256, 256, 128), at_rows(y * 512 + sx * 256 + sc * 128, 128, 128)]
+    s_up, s_down = links.base("up", 4), links.base("down", 4)
+    own_up = local(6, w1_in.at[:, at_rows(q * 256, 256, 128)], up_shard(x, c))
+    own_down = local(7, w2_in.at[at_rows(q * 256, 256, 128), :], down_shard(x, c))
+    own_up.start()
+    own_down.start()
+
+    def part_up(dx, dc):
+        tx, tc, rel = (x + dx) % 2, (c + dc) % 2, 2 * dx + dc
+        to = place(y, tx, tc, z)
+        links.put(w1_in.at[:, at_rows((2 * tx + tc) * 256, 256, 128)], up_shard(x, c), s_up + rel, s_up + rel, to)
+
+    def part_down(dx, dc):
+        tx, tc, rel = (x + dx) % 2, (c + dc) % 2, 2 * dx + dc
+        to = place(y, tx, tc, z)
+        links.put(w2_in.at[at_rows((2 * tx + tc) * 256, 256, 128), :], down_shard(x, c), s_down + rel, s_down + rel, to)
+
+    def wait_parts(shard, base):
+        for dx, dc in ((0, 1), (1, 0), (1, 1)):
+            links.wait(shard((x + dx) % 2, (c + dc) % 2), base + 2 * dx + dc, to_c)
+
+    class Fan:
+        def __init__(self, key, piece, arrived):
+            self.piece, self.arrived = piece, arrived
+            self.many = len(piece(0))
+            self.got = [links.base((key, "got", n), 4) for n in range(self.many)]
+            self.sent = [links.base((key, "sent", n), 3) for n in range(self.many)]
+
+        def push(self, slot, o, to):
+            for n in range(self.many):
+                def make(n=n):
+                    ref = self.piece(o)[n]
+                    return ref, ref, self.sent[n] + slot, self.got[n] + o, to, None
+
+                links.start(make)
+
+        def take(self, o):
+            for n, ref in enumerate(self.piece(o)):
+                links.wait(ref, self.got[n] + o, to_z1)
+
+        def begin(self):
+            self.push(1, z, to_z1)
+            self.push(0, z, to_z2)
+            self.arrived(z)
+
+        def far(self):
+            self.take(z2)
+            self.push(2, z2, to_z1)
+            self.arrived(z2)
+
+        def pair(self):
+            self.take(z1)
+            self.arrived(z1)
+
+        def diagonal(self):
+            self.take(z3)
+            self.arrived(z3)
+
+    class Line:
+        def __init__(self, key, piece, arrived):
+            self.piece, self.arrived = piece, arrived
+            self.many = len(piece(0))
+            self.got = [links.base((key, "got", n), 4) for n in range(self.many)]
+            self.sent = [links.base((key, "sent", n), 8) for n in range(self.many)]
+
+        def push(self, upward, o, there):
+            onward = z < 3 if upward else z > 0
+            to = place(y, x, c, jnp.minimum(z + 1, 3) if upward else jnp.maximum(z - 1, 0))
+            to = (jnp.where(onward, to[0], to_c[0]), to[1])
+            for n, ref in enumerate(self.piece(o)):
+                links.put(ref, ref, self.sent[n] + 4 * upward + o, self.got[n] + o, to, jnp.logical_and(there, onward))
+
+        def begin(self):
+            self.push(1, z, z >= 0)
+            self.push(0, z, z >= 0)
+            self.arrived(z, None)
+
+        def step(self, far):
+            for upward in (1, 0):
+                o = z - far if upward else z + far
+                there = o >= 0 if upward else o < 4
+                o = jnp.clip(o, 0, 3)
+
+                @pl.when(there)
+                def _():
+                    for n, ref in enumerate(self.piece(o)):
+                        links.wait(ref, self.got[n] + o, to_z1)
+
+                self.push(upward, o, there)
+                self.arrived(o, there)
+
+    attn_at = (qkv_at, wo_at)
+
+    def attn_whole(o):
+        return (
+            qkv.at[at_rows(r * 256, 256, 256), at_rows(o * 384, 384, 128)],
+            wo.at[at_rows(o * 128, 128, 128), at_rows(r * 256, 256, 256)],
+        )
+
+    s_first = [links.base(("first", n), 8) for n in range(2)]
+    s_own = [links.base(("own", n), 8) for n in range(2)]
+    s_fwd = [links.base(("fwd", n), 8) for n in range(2)]
+    to_first, to_second = (to_x, to_y), (to_y, to_x)
+    r_first, r_second = (r_x, r_y), (r_y, r_x)
+
+    def attn_arrived(o, there):
+        for n, at in enumerate(attn_at):
+            for cs in range(2):
+                ref, sem = at(r, o, cs), o * 2 + cs
+                links.put(ref, ref, s_first[n] + sem, s_first[n] + sem, to_first[cs], there)
+        for n, at in enumerate(attn_at):
+            for cs in range(2):
+                ref, sem = at(r, o, cs), o * 2 + cs
+                links.put(ref, ref, s_own[n] + sem, s_own[n] + sem, to_second[cs], there)
+
+    def attn_forward(o, there=None):
+        for n, at in enumerate(attn_at):
+            for cs in range(2):
+                ref, sem = at(r_first[cs], o, cs), o * 2 + cs
+
+                def arrive(n=n, ref=ref, sem=sem):
+                    links.wait(ref, s_first[n] + sem, to_x)
+
+                arrive() if there is None else pl.when(there)(arrive)
+                links.put(ref, ref, s_fwd[n] + sem, s_fwd[n] + sem, to_second[cs], there)
+
+    def attn_forward_far(far):
+        attn_forward(jnp.clip(z - far, 0, 3), z >= far)
+        attn_forward(jnp.clip(z + far, 0, 3), z + far < 4)
+
+    def attn_finish():
+        for o in range(4):
+            for n, at in enumerate(attn_at):
+                for cs in range(2):
+                    sem = o * 2 + cs
+                    links.wait(at(r_second[cs], o, cs), s_own[n] + sem, to_x)
+                    links.wait(at(r_xy, o, cs), s_fwd[n] + sem, to_x)
+
+    attn_line = Line("attn", lambda o: attn_whole(o), attn_arrived)
+    up_at = lambda yy, o: up.at[at_rows(yy * 512, 512, 512), at_rows(o * 256, 256, 256)]
+    down_at = lambda yy, o: down.at[at_rows(o * 256, 256, 256), at_rows(yy * 512, 512, 512)]
+    s_upy, s_downy = links.base("upy", 4), links.base("downy", 4)
+
+    def across(at, base):
+        return lambda o: links.start(lambda: (at(y, o), at(y, o), base + o, base + o, to_y, None))
+
+    up_fan = Fan("upf", lambda o: (up_at(y, o),), across(up_at, s_upy))
+    down_fan = Fan("downf", lambda o: (down_at(y, o),), across(down_at, s_downy))
+
+    lse[...] = jnp.zeros_like(lse)
+    for one in own_qkv:
+        one.wait()
+    own_wo.wait()
+    for t in range(3):
+        links.wait(qkv_spot(t, 1 - c), s_pc3 + t, to_c)
+    links.wait(wo_at(r, z, 1 - c), s_pc + 1, to_c)
+    def spread_start(key, ref):
+        base = links.base(("spread", key), 3)
+        links.start(lambda: (block_at(ref, q), block_at(ref, q), base, base, to_x, None))
+        links.start(lambda: (block_at(ref, q), block_at(ref, q), base + 1, base + 1, to_c, None))
+
+    def spread_forward(key, ref):
+        base = links.base(("spread", key), 3)
+        far = lambda: block_at(ref, 2 * (1 - x) + c)
+        links.wait(far(), base, to_x)
+        links.start(lambda: (far(), far(), base + 2, base + 2, to_c, None))
+
+    def spread_wait_near(key, ref):
+        links.wait(block_at(ref, 2 * x + 1 - c), links.base(("spread", key), 3) + 1, to_c)
+
+    def spread_wait_far(key, ref):
+        links.wait(block_at(ref, 2 * (1 - x) + 1 - c), links.base(("spread", key), 3) + 2, to_c)
+
+    attn_line.begin()
     norm_in[0:2, :] = gain_in[...].astype(F32)
     norm_in[2:6, :] = shift_in[...].astype(F32)
     norm_in[6:8, :] = jnp.zeros((2, 128), F32)
@@ -439,6 +651,8 @@
     mask_in[1] = hidden[1:2]
     number = tok_raw.shape[0]
     full_rows = number // 16 * 16
+    for one in raw_copies:
+        one.wait()
     for one_raw, one_in in ((tok_raw, tok_in), (cot_raw, cot_in)):
         for i in range(2):
             one_in[i, full_rows:Q, :] = jnp.zeros((Q - full_rows, 1024), BF)
@@ -454,212 +668,6 @@
     for one in own_small:
         one.start()
 
-    def move_tokens(key, source, target_at, at):
-        base, got = links.base((key, "sent"), 2), links.base((key, "got"), 2)
-        target = target_at(z // 2)
-        stay = c == z // 2
-        rows = at_rows((z % 2) * Q, SENT, 16)
-        for i in range(2):
-            here = jnp.logical_and(stay, z % 2 == i)
-            to = place(y, x, z // 2, 2 * c + i)
-            to = (jnp.where(here, place(y, x, 1 - c, z)[0], to[0]), to[1])
-            mine = source.at[i, pl.ds(0, SENT)]
-            links.put(mine, target.at[rows], base + i, got + z % 2, to, jnp.logical_not(here))
-
-            @pl.when(here)
-            def _(mine=mine):
-                local(at, mine, target.at[rows]).start()
-
-    def wait_tokens(key, source, target_at, at):
-        got = links.base((key, "got"), 2)
-        target = target_at(c)
-        stay = c == z // 2
-        for j in range(2):
-            here = jnp.logical_and(stay, z % 2 == j)
-
-            @pl.when(here)
-            def _(j=j):
-                local(at, source.at[j, pl.ds(0, SENT)], target.at[pl.ds(j * Q, SENT)]).wait()
-
-            @pl.when(jnp.logical_not(here))
-            def _(j=j):
-                links.wait(target.at[pl.ds(j * Q, SENT)], got + j, to_c)
-
-    up_shard = lambda sx, sc: up.at[at_rows(y * 512 + sx * 256 + sc * 128, 128, 128), at_rows(z * 256, 256, 128)]
-    down_shard = lambda sx, sc: down.at[at_rows(z * 256, 256, 128), at_rows(y * 512 + sx * 256 + sc * 128, 128, 128)]
-    s_up, s_down = links.base("up", 4), links.base("down", 4)
-    own_up = local(6, w1_in.at[:, at_rows(q * 256, 256, 128)], up_shard(x, c))
-    own_down = local(7, w2_in.at[at_rows(q * 256, 256, 128), :], down_shard(x, c))
-    own_up.start()
-    own_down.start()
-
-    def part_up(dx, dc):
-        tx, tc, rel = (x + dx) % 2, (c + dc) % 2, 2 * dx + dc
-        to = place(y, tx, tc, z)
-        links.put(w1_in.at[:, at_rows((2 * tx + tc) * 256, 256, 128)], up_shard(x, c), s_up + rel, s_up + rel, to)
-
-    def part_down(dx, dc):
-        tx, tc, rel = (x + dx) % 2, (c + dc) % 2, 2 * dx + dc
-        to = place(y, tx, tc, z)
-        links.put(w2_in.at[at_rows((2 * tx + tc) * 256, 256, 128), :], down_shard(x, c), s_down + rel, s_down + rel, to)
-
-    def wait_parts(shard, base):
-        for dx, dc in ((0, 1), (1, 0), (1, 1)):
-            links.wait(shard((x + dx) % 2, (c + dc) % 2), base + 2 * dx + dc, to_c)
-
-    class Fan:
-        def __init__(self, key, piece, arrived):
-            self.piece, self.arrived = piece, arrived
-            self.many = len(piece(0))
-            self.got = [links.base((key, "got", n), 4) for n in range(self.many)]
-            self.sent = [links.base((key, "sent", n), 3) for n in range(self.many)]
-
-        def push(self, slot, o, to):
-            for n in range(self.many):
-                def make(n=n):
-                    ref = self.piece(o)[n]
-                    return ref, ref, self.sent[n] + slot, self.got[n] + o, to, None
-
-                links.start(make)
-
-        def take(self, o):
-            for n, ref in enumerate(self.piece(o)):
-                links.wait(ref, self.got[n] + o, to_z1)
-
-        def begin(self):
-            self.push(1, z, to_z1)
-            self.push(0, z, to_z2)
-            self.arrived(z)
-
-        def far(self):
-            self.take(z2)
-            self.push(2, z2, to_z1)
-            self.arrived(z2)
-
-        def pair(self):
-            self.take(z1)
-            self.arrived(z1)
-
-        def diagonal(self):
-            self.take(z3)
-            self.arrived(z3)
-
-    class Line:
-        def __init__(self, key, piece, arrived):
-            self.piece, self.arrived = piece, arrived
-            self.many = len(piece(0))
-            self.got = [links.base((key, "got", n), 4) for n in range(self.many)]
-            self.sent = [links.base((key, "sent", n), 8) for n in range(self.many)]
-
-        def push(self, upward, o, there):
-            onward = z < 3 if upward else z > 0
-            to = place(y, x, c, jnp.minimum(z + 1, 3) if upward else jnp.maximum(z - 1, 0))
-            to = (jnp.where(onward, to[0], to_c[0]), to[1])
-            for n, ref in enumerate(self.piece(o)):
-                links.put(ref, ref, self.sent[n] + 4 * upward + o, self.got[n] + o, to, jnp.logical_and(there, onward))
-
-        def begin(self):
-            self.push(1, z, z >= 0)
-            self.push(0, z, z >= 0)
-            self.arrived(z, None)
-
-        def step(self, far):
-            for upward in (1, 0):
-                o = z - far if upward else z + far
-                there = o >= 0 if upward else o < 4
-                o = jnp.clip(o, 0, 3)
-
-                @pl.when(there)
-                def _():
-                    for n, ref in enumerate(self.piece(o)):
-                        links.wait(ref, self.got[n] + o, to_z1)
-
-                self.push(upward, o, there)
-                self.arrived(o, there)
-
-    attn_at = (qkv_at, wo_at)
-
-    def attn_whole(o):
-        return (
-            qkv.at[at_rows(r * 256, 256, 256), at_rows(o * 384, 384, 128)],
-            wo.at[at_rows(o * 128, 128, 128), at_rows(r * 256, 256, 256)],
-        )
-
-    s_first = [links.base(("first", n), 8) for n in range(2)]
-    s_own = [links.base(("own", n), 8) for n in range(2)]
-    s_fwd = [links.base(("fwd", n), 8) for n in range(2)]
-    to_first, to_second = (to_x, to_y), (to_y, to_x)
-    r_first, r_second = (r_x, r_y), (r_y, r_x)
-
-    def attn_arrived(o, there):
-        for n, at in enumerate(attn_at):
-            for cs in range(2):
-                ref, sem = at(r, o, cs), o * 2 + cs
-                links.put(ref, ref, s_first[n] + sem, s_first[n] + sem, to_first[cs], there)
-        for n, at in enumerate(attn_at):
-            for cs in range(2):
-                ref, sem = at(r, o, cs), o * 2 + cs
-                links.put(ref, ref, s_own[n] + sem, s_own[n] + sem, to_second[cs], there)
-
-    def attn_forward(o, there=None):
-        for n, at in enumerate(attn_at):
-            for cs in range(2):
-                ref, sem = at(r_first[cs], o, cs), o * 2 + cs
-
-                def arrive(n=n, ref=ref, sem=sem):
-                    links.wait(ref, s_first[n] + sem, to_x)
-
-                arrive() if there is None else pl.when(there)(arrive)
-                links.put(ref, ref, s_fwd[n] + sem, s_fwd[n] + sem, to_second[cs], there)
-
-    def attn_forward_far(far):
-        attn_forward(jnp.clip(z - far, 0, 3), z >= far)
-        attn_forward(jnp.clip(z + far, 0, 3), z + far < 4)
-
-    def attn_finish():
-        for o in range(4):
-            for n, at in enumerate(attn_at):
-                for cs in range(2):
-                    sem = o * 2 + cs
-                    links.wait(at(r_second[cs], o, cs), s_own[n] + sem, to_x)
-                    links.wait(at(r_xy, o, cs), s_fwd[n] + sem, to_x)
-
-    attn_line = Line("attn", lambda o: attn_whole(o), attn_arrived)
-    up_at = lambda yy, o: up.at[at_rows(yy * 512, 512, 512), at_rows(o * 256, 256, 256)]
-    down_at = lambda yy, o: down.at[at_rows(o * 256, 256, 256), at_rows(yy * 512, 512, 512)]
-    s_upy, s_downy = links.base("upy", 4), links.base("downy", 4)
-
-    def across(at, base):
-        return lambda o: links.start(lambda: (at(y, o), at(y, o), base + o, base + o, to_y, None))
-
-    up_fan = Fan("upf", lambda o: (up_at(y, o),), across(up_at, s_upy))
-    down_fan = Fan("downf", lambda o: (down_at(y, o),), across(down_at, s_downy))
-
-    lse[...] = jnp.zeros_like(lse)
-    for one in own_qkv:
-        one.wait()
-    own_wo.wait()
-    for t in range(3):
-        links.wait(qkv_spot(t, 1 - c), s_pc3 + t, to_c)
-    links.wait(wo_at(r, z, 1 - c), s_pc + 1, to_c)
-    def spread_start(key, ref):
-        base = links.base(("spread", key), 3)
-        links.start(lambda: (block_at(ref, q), block_at(ref, q), base, base, to_x, None))
-        links.start(lambda: (block_at(ref, q), block_at(ref, q), base + 1, base + 1, to_c, None))
-
-    def spread_forward(key, ref):
-        base = links.base(("spread", key), 3)
-        far = lambda: block_at(ref, 2 * (1 - x) + c)
-        links.wait(far(), base, to_x)
-        links.start(lambda: (far(), far(), base + 2, base + 2, to_c, None))
-
-    def spread_wait_near(key, ref):
-        links.wait(block_at(ref, 2 * x + 1 - c), links.base(("spread", key), 3) + 1, to_c)
-
-    def spread_wait_far(key, ref):
-        links.wait(block_at(ref, 2 * (1 - x) + 1 - c), links.base(("spread", key), 3) + 2, to_c)
-
-    attn_line.begin()
     attn_line.step(1)
     attn_forward(z)
     attn_line.step(2)
@@ -717,6 +725,7 @@
     lane = lax.broadcasted_iota(jnp.int32, (1, 128), 1)
     first_head = lane < 64
     zero = jnp.zeros((), BF)
+    factor = jnp.asarray(HD ** (-0.5), BF)
 
     @pl.loop(0, 4)
     def _(zz):
@@ -729,7 +738,7 @@
             outs = []
             for hh in range(2):
                 own = jnp.where(first_head if hh == 0 else jnp.logical_not(first_head), pair, zero)
-                scores = mm(own, keys, NT) * (HD ** (-0.5)) + hidden_key
+                scores = mm(own * factor, keys, NT) + hidden_key
                 highest = jnp.max(scores, axis=-1, keepdims=True)
                 exponent = jnp.exp(scores - highest)
                 total = jnp.sum(exponent, axis=-1, keepdims=True)
@@ -1231,9 +1240,6 @@
     front_part(1 - c, s_far)
     links.put(s_far, g_n1, s_gn1, s_gn1, to_c)
     front_part(c, part)
-    for o in (z1, z2):
-        red_qkv.middle(o)
-    red_qkv.pair_far()
     links.wait(g_n1, s_gn1, to_c)
     links.copy(s_mid, b_mid, s_bmid, s_bmid, to_x).wait_send()
     links.drop(s_bmid)
@@ -1266,6 +1272,9 @@
 
         links.start(make)
     send_home("home", s_mid, grad_out, 10)
+    for o in (z1, z2):
+        red_qkv.middle(o)
+    red_qkv.pair_far()
     red_qkv.pair_near()
     red_qkv.middle(z)
     red_qkv.far()
@@ -1341,7 +1350,7 @@
     low = lambda *dims: pltpu.VMEM(dims, BF)
     wide = lambda *dims: pltpu.VMEM(dims, F32)
     scratch = [
-        low(2, Q, 1024), low(2, Q, 1024), wide(2, 1, FULL), wide(8, 128), wide(8, 128),
+        low(*operands[0].shape), low(*operands[0].shape), low(2, Q, 1024), low(2, Q, 1024), wide(2, 1, FULL), wide(8, 128), wide(8, 128),
         low(HALF, 1024), low(4 * HALF, 1024), wide(2, 2, 1, FULL), wide(8, 8, 128), wide(4, 8, 128),
         low(1024, 1536), low(512, 1024), low(1024, 1024), low(1024, 1024),
         low(FULL, 1024), low(FULL, 1536), wide(FULL, 128), low(FULL, 512), wide(HALF, 1024),
@@ -1356,12 +1365,12 @@
         *[low(HALF, 1024)] * 10,
         wide(48, 1024), wide(8, 1024), wide(8, 8, 128), wide(8, 128),
         wide(8, 1024), wide(8, 512), wide(8, 512), wide(4, 8, 128), wide(4, 8, 128), wide(8, 128),
-        pltpu.SemaphoreType.DMA((19,)), pltpu.SemaphoreType.DMA((130,)), pltpu.SemaphoreType.DMA((212,)),
+        pltpu.SemaphoreType.DMA((21,)), pltpu.SemaphoreType.DMA((130,)), pltpu.SemaphoreType.DMA((212,)),
     ]
     return pl.pallas_call(
         layer_kernel,
         out_shape=outs,
-        in_specs=[vmem] * 7 + [hbm] * 4,
+        in_specs=[hbm] * 2 + [vmem] * 5 + [hbm] * 4,
         out_specs=[hbm] * 8,
         scratch_shapes=scratch,
         compiler_params=pltpu.CompilerParams(collective_id=0, has_side_effects=True, vmem_limit_bytes=67043328),

time: 212 us -> 210 us (level)
  no operation moved by 1% of the time
where the time goes in v3:
time: 210 us; the launch traced here: 209 us
  Pallas kernels  209 us (100%)
    pallas_call x1, Pallas kernels, layer_call(): pl.pallas_call(layer_kernel, out_shape=outs, in_specs=[hbm] * 2 + [vmem]...  205 us

profile of v3, /device:TPU:1, one launch (start us, length us, event | category | flops | bytes accessed | tf_op | source)
XLA Modules:
  0.0 209.5 jit_solution(6704648460141352327)
XLA Ops:
  0.6 205.0 %layer.1 = (bf16[2,160,1024]{2,1,0:T(8,128)(2,1)}, bf16[2,160,1024]{2,1,0:T(8,128)(2,1)}, bf16[4,128,256]{2,1,0:T(8,128)(2,1)}, bf16[4,256,128]{2,1,0:T(8,128)(2...) custom-call(bf16[146,2,1024]{2,1,0:T(2,128)(2,1)} %tok_src.1, ...), custom_call_target="tpu_custom_call" | custom-call | tf_op jit(solution)/shard_map/layer/pallas_call | solution.py:1370
  205.7 3.8 %finish.1 = (bf16[146,2,1024]{2,1,0:T(2,128)(2,1)}, f32[146,2,1024]{2,1,0:T(2,128)}, f32[2,128]{1,0:T(2,128)}, f32[4,128]{1,0:T(4,128)}, f32[3,128,256]{2,1,0:T(...) custom-call(bf16[2,160,1024]{2,1,0:T(8,128)(2,1)} %get-tuple-element, ...), custom_call_target="tpu_custom_call" | custom-call | tf_op jit(solution)/shard_map/finish/pallas_call | solution.py:1406
